TPU v7x, 32 devices: a whole 2x2x4 slice. The times are simulated.
32 devices in a mesh: ep: 16 (over z, y, x), half: 2 (over core).
Axes of the slice: x: 2, y: 2, z: 4, core: 2. Of those that a mesh axis runs over, the one named last changes fastest.
Arguments:
- tokens: bfloat16 [2048, 2048], P('ep', 'half'), may hold values from -6 to 6
- gate_weights: float32 [2048, 8], P('ep'), may hold values from 0.05 to 0.3
- expert_ids: int32 [2048, 8], P('ep'), may hold values from 0 to 15, all different within a row; in each aligned block of 128 rows (0 to 127, 128 to 255, ...) at most 80 rows name the same one
- w_gate: bfloat16 [16, 2048, 768], P('ep', None, 'half'), may hold values from -0.125 to 0.125
- w_up: bfloat16 [16, 2048, 768], P('ep', None, 'half'), may hold values from -0.125 to 0.125
- w_down: bfloat16 [16, 768, 2048], P('ep', 'half'), may hold values from -0.21875 to 0.21875
Outputs:
- mixed: bfloat16 [2048, 2048], P('ep', 'half')
Inputs may be any that keep to these rules, and one draw needn't show every extreme that they name: `expert_ids`: each row names 8 different experts. Within the rows of one device (aligned blocks of 128 rows) no expert is named by more than 80 rows, and in every draw some expert is named by exactly 80 rows of some block.
All inputs are finite; a program needn't handle non-finite values.
Results may differ from a plain program's by a relative error of at most 0.0085.
Values may be sent and summed in bfloat16 or wider, within the bound.
A program may use at most 64 MiB of HBM per device.

v0:
```python
import functools

import jax
import jax.numpy as jnp
from jax import lax
from jax.experimental import pallas as pl
from jax.experimental.pallas import tpu as pltpu
from jax.sharding import PartitionSpec as P

MESH = pl.DeviceIdType.MESH


def slots(tokens, gate_weights, expert_ids, w_gate, w_up, w_down):
    tok_dev, half_width = tokens.shape
    top = expert_ids.shape[1]
    local_experts = w_gate.shape[0]
    experts = local_experts * lax.axis_size("ep")
    capacity = min(tok_dev, max(2, 5 * tok_dev * top // (4 * experts)))
    flat_ids = expert_ids.reshape(-1)
    columns = jnp.arange(experts, dtype=jnp.int32)
    onehot = (flat_ids[:, None] == columns[None, :]).astype(jnp.int32)
    ranks = jnp.sum((jnp.cumsum(onehot, axis=0) - onehot) * onehot, axis=1)
    slot = flat_ids * capacity + ranks
    token_of_pair = jnp.arange(tok_dev * top, dtype=jnp.int32) // top
    token_table = jnp.zeros((experts * capacity,), jnp.int32).at[slot].set(token_of_pair)
    filled = (
        jnp.zeros((experts * capacity,), jnp.bfloat16)
        .at[slot]
        .set(jnp.ones((tok_dev * top,), jnp.bfloat16))
    )
    outgoing = (tokens[token_table] * filled[:, None]).reshape(experts, capacity, half_width)
    received = lax.all_to_all(outgoing, "ep", split_axis=0, concat_axis=0, tiled=True)
    count = received.shape[1]
    whole = lax.all_gather(received, "half", axis=2, tiled=True)
    width = whole.shape[2]
    grouped = whole.reshape(-1, local_experts, count, width)
    gate = jnp.einsum("secd,edf->secf", grouped, w_gate, preferred_element_type=jnp.float32)
    up = jnp.einsum("secd,edf->secf", grouped, w_up, preferred_element_type=jnp.float32)
    hidden = (jax.nn.silu(gate) * up).astype(jnp.bfloat16)
    partial_out = jnp.einsum("secf,efd->secd", hidden, w_down, preferred_element_type=jnp.float32)
    partial_out = partial_out.astype(jnp.bfloat16).reshape(experts, count, width)
    widened = lax.optimization_barrier(partial_out).astype(jnp.float32)
    summed = lax.psum_scatter(widened.astype(jnp.bfloat16), "half", scatter_dimension=2, tiled=True)
    answer = lax.all_to_all(summed, "ep", split_axis=0, concat_axis=0, tiled=True)
    picked = answer.reshape(experts * capacity, -1)[slot].reshape(tok_dev, top, -1)
    slot_out = picked.astype(jnp.float32)
    mixed = jnp.einsum("tk,tkx->tx", gate_weights, slot_out)
    return mixed.astype(jnp.bfloat16)


def kernel(nz, tok_ref, gw_ref, ids_ref, wg_ref, wu_ref, wd_ref, out_ref,
           xg, wgu, wdn, pa, pb, da, db, rxa, rxb, rya, ryb, own, zs, rz, fin, rfin,
           load_sem, pre_sem, wsend, wrecv, zsend, zrecv, xsend, xrecv, ysend, yrecv,
           fxsend, fxrecv, fysend, fyrecv,
           esend, erecv, dsend, drecv, csend, crecv, qsend, qrecv, fsend, frecv):
    ep = lax.axis_index("ep")
    core = lax.axis_index("half")
    x, y, z = ep % 2, (ep // 2) % 2, ep // 4
    rows, width = out_ref.shape[0] // 2, wg_ref.shape[1]
    half, ff = width // 2, wg_ref.shape[2]
    other = {"half": 1 - core}
    xn = {"ep": z * 4 + y * 2 + (1 - x)}
    yn = {"ep": z * 4 + (1 - y) * 2 + x}

    def zn(to):
        return {"ep": to * 4 + y * 2 + x}

    def send(src, dst, s, r, to):
        return pltpu.make_async_remote_copy(
            src_ref=src, dst_ref=dst, send_sem=s, recv_sem=r, device_id=to, device_id_type=MESH
        )

    def at(d):
        bit, to = 1, z
        while bit < nz:
            if d & bit:
                to = to + bit - 2 * bit * ((z // bit) % 2)
            bit *= 2
        return to

    loads = [
        pltpu.make_async_copy(wg_ref.at[0], wgu.at[0, :, pl.ds(0, ff)], load_sem.at[0]),
        pltpu.make_async_copy(wu_ref.at[0], wgu.at[0, :, pl.ds(ff, ff)], load_sem.at[1]),
        pltpu.make_async_copy(wd_ref.at[0], wdn.at[pl.ds(0, ff)], load_sem.at[2]),
    ]
    mine = pltpu.make_async_copy(
        tok_ref.at[pl.ds(core * rows, rows)],
        xg.at[0, z, :, pl.ds(pl.multiple_of(core * half, 128), half)],
        load_sem.at[3],
    )
    mine.start()
    for load in loads:
        load.start()

    expert_at = lax.broadcasted_iota(jnp.int32, (128, 2 * rows), 0) % 64
    spread = jnp.zeros((128, 2 * rows), jnp.float32)
    for k in range(ids_ref.shape[0]):
        spread += jnp.where(expert_at == ids_ref[k : k + 1, :], gw_ref[k : k + 1, :], 0.0)
    spread = jnp.transpose(spread)
    spread = jnp.where(core == 0, spread[:rows], spread[rows:])
    lane = lax.broadcasted_iota(jnp.int32, (rows, 128), 1)
    upper = spread.astype(jnp.bfloat16).astype(jnp.float32)
    both = jnp.where(lane < 64, upper, spread - upper)
    xg[0, z, :, width : width + 128] = both.astype(jnp.bfloat16)

    barrier = pltpu.get_barrier_semaphore()
    partners = [other, xn, yn] + [zn(at(d)) for d in range(1, nz)]
    for partner in partners:
        pl.semaphore_signal(barrier, inc=1, device_id=partner, device_id_type=MESH)
    pl.semaphore_wait(barrier, len(partners))

    pre = send(
        tok_ref.at[pl.ds((1 - core) * rows, rows)],
        xg.at[0, z, :, pl.ds(pl.multiple_of(core * half, 128), half)],
        pre_sem.at[0], pre_sem.at[1], other,
    )
    pre.start()
    swaps = [
        send(wg_ref.at[0], wgu.at[1, :, pl.ds(0, ff)], wsend.at[0], wrecv.at[0], other),
        send(wu_ref.at[0], wgu.at[1, :, pl.ds(ff, ff)], wsend.at[1], wrecv.at[1], other),
        send(wd_ref.at[0], wdn.at[pl.ds(ff, ff)], wsend.at[2], wrecv.at[2], other),
    ]
    mine.wait()
    pre.wait_recv()
    sent = [pre]

    def go(copy):
        copy.start()
        sent.append(copy)
        return copy

    first, last = pl.ds(0, half), pl.ds(half, half + 128)
    xs, ys, fx, fy, zc = {}, {}, {}, {}, {}

    def column(d):
        b = xg.at[0, at(d)]
        for p, cols in enumerate((first, last)):
            xs[d, p] = go(send(b.at[:, cols], xg.at[1, at(d), :, cols],
                               xsend.at[p, d], xrecv.at[p, d], xn))
        for p, cols in ((1, last), (0, first)):
            ys[d, p] = go(send(b.at[:, cols], xg.at[2, at(d), :, cols],
                               ysend.at[p, d], yrecv.at[p, d], yn))

    def forward(d):
        ys[d, 1].wait_recv()
        fx[d] = go(send(xg.at[2, at(d), :, last], xg.at[3, at(d), :, last],
                        fxsend.at[d], fxrecv.at[d], xn))
        xs[d, 0].wait_recv()
        fy[d] = go(send(xg.at[1, at(d), :, first], xg.at[3, at(d), :, first],
                        fysend.at[d], fyrecv.at[d], yn))

    hops = sorted(range(1, nz), key=lambda d: bin(d ^ (d >> 1)).count("1"))
    for d in hops:
        zc[d] = go(send(xg.at[0, z], xg.at[0, z], zsend.at[d - 1], zrecv.at[d - 1], zn(at(d))))
    column(0)
    for swap in swaps:
        go(swap)
    forward(0)
    for place, d in enumerate(hops):
        zc[d].wait_recv()
        column(d)
        if place:
            forward(hops[place - 1])

    many = nz * rows

    def expert(g):
        lanes = lax.broadcasted_iota(jnp.int32, (many, 128), 1)
        table = xg[g, :, :, width : width + 128].reshape(many, 128).astype(jnp.float32)
        weight = jnp.sum(jnp.where(lanes % 64 == ep, table, 0.0), axis=1, keepdims=True)
        rows_in = xg[g, :, :, 0:width].reshape(many, width)
        parts = []
        for side in range(2):
            gu = jnp.dot(rows_in, wgu[side], preferred_element_type=jnp.float32)
            gate, up = gu[:, :ff], gu[:, ff:]
            hid = gate / (1.0 + jnp.exp(-gate)) * up * weight
            parts.append(hid.astype(jnp.bfloat16))
        hidden = jnp.concatenate(parts, axis=1)
        for to, start in ((pa, 0), (pb, half)):
            o = jnp.dot(hidden, wdn[:, start : start + half], preferred_element_type=jnp.float32)
            to[g] = o.astype(jnp.bfloat16).reshape(nz, rows, half)

    for load in loads:
        load.wait()
    for swap in swaps:
        swap.wait_recv()
    expert(0)
    forward(hops[-1])
    for d in range(nz):
        xs[d, 1].wait_recv()
    expert(1)
    early_x = go(send(pb.at[1], rxb, esend.at[0], erecv.at[0], xn))
    for d in range(nz):
        ys[d, 0].wait_recv()
    expert(2)
    early_y = go(send(pa.at[2], rya, esend.at[1], erecv.at[1], yn))
    for d in range(nz):
        fx[d].wait_recv()
        fy[d].wait_recv()
    expert(3)
    order = hops[::-1] + [0]
    dx, dy, cx, cy, zq = {}, {}, {}, {}, {}
    f32 = jnp.float32

    def corner(d):
        dy[d] = go(send(pa.at[3, at(d)], da.at[at(d)], dsend.at[0, d], drecv.at[0, d], yn))
        dx[d] = go(send(pb.at[3, at(d)], db.at[at(d)], dsend.at[1, d], drecv.at[1, d], xn))

    def edge(d):
        dy[d].wait_recv()
        pa[1, at(d)] = (pa[1, at(d)].astype(f32) + da[at(d)].astype(f32)).astype(jnp.bfloat16)
        cx[d] = go(send(pa.at[1, at(d)], rxa.at[at(d)], csend.at[0, d], crecv.at[0, d], xn))
        dx[d].wait_recv()
        pb[2, at(d)] = (pb[2, at(d)].astype(f32) + db[at(d)].astype(f32)).astype(jnp.bfloat16)
        cy[d] = go(send(pb.at[2, at(d)], ryb.at[at(d)], csend.at[1, d], crecv.at[1, d], yn))

    def home(d):
        cx[d].wait_recv()
        cy[d].wait_recv()
        sums = []
        for p, u, v in ((pa, rxa, rya), (pb, rxb, ryb)):
            sums.append(p[0, at(d)].astype(f32) + u[at(d)].astype(f32) + v[at(d)].astype(f32))
        if d:
            zs[d - 1, :, 0:half] = sums[0].astype(jnp.bfloat16)
            zs[d - 1, :, half:width] = sums[1].astype(jnp.bfloat16)
            zq[d] = go(send(zs.at[d - 1], rz.at[d - 1], qsend.at[d - 1], qrecv.at[d - 1], zn(at(d))))
        else:
            own[:, 0:half] = sums[0]
            own[:, half:width] = sums[1]

    corner(order[0])
    corner(order[1])
    for place, d in enumerate(order):
        edge(d)
        if place + 2 < len(order):
            corner(order[place + 2])
        if place == 1:
            early_x.wait_recv()
            early_y.wait_recv()
        if place:
            home(order[place - 1])
    home(order[-1])
    total = own[...]
    for d in range(1, nz):
        zq[d].wait_recv()
        total += rz[d - 1].astype(f32)
    total = total.astype(jnp.bfloat16)
    fin[0] = total[:, 0:half]
    fin[1] = total[:, half:width]
    swap = go(send(fin.at[1 - core], rfin, fsend, frecv, other))
    out_ref[pl.ds(core * rows, rows), :] = fin[core]
    swap.wait_recv()
    out_ref[pl.ds((1 - core) * rows, rows), :] = rfin[...]
    for copy in sent:
        copy.wait_send()


def multicast(tokens, gate_weights, expert_ids, w_gate, w_up, w_down):
    tok_dev, half = tokens.shape
    nz = lax.axis_size("ep") // 4
    rows, width, ff = tok_dev // 2, w_gate.shape[1], w_gate.shape[2]
    bf, dma = jnp.bfloat16, pltpu.SemaphoreType.DMA
    vmem, hbm = pl.BlockSpec(memory_space=pltpu.VMEM), pl.BlockSpec(memory_space=pl.ANY)
    return pl.pallas_call(
        functools.partial(kernel, nz),
        out_shape=jax.ShapeDtypeStruct((tok_dev, half), bf),
        in_specs=[vmem, vmem, vmem, hbm, hbm, hbm],
        out_specs=vmem,
        scratch_shapes=[
            pltpu.VMEM((4, nz, rows, width + 128), bf),
            pltpu.VMEM((2, width, 2 * ff), bf),
            pltpu.VMEM((2 * ff, width), bf),
            pltpu.VMEM((4, nz, rows, half), bf),
            pltpu.VMEM((4, nz, rows, half), bf),
            pltpu.VMEM((nz, rows, half), bf),
            pltpu.VMEM((nz, rows, half), bf),
            pltpu.VMEM((nz, rows, half), bf),
            pltpu.VMEM((nz, rows, half), bf),
            pltpu.VMEM((nz, rows, half), bf),
            pltpu.VMEM((nz, rows, half), bf),
            pltpu.VMEM((rows, width), jnp.float32),
            pltpu.VMEM((nz - 1, rows, width), bf),
            pltpu.VMEM((nz - 1, rows, width), bf),
            pltpu.VMEM((2, rows, half), bf),
            pltpu.VMEM((rows, half), bf),
            dma((4,)), dma((2,)), dma((3,)), dma((3,)),
            dma((nz - 1,)), dma((nz - 1,)),
            dma((2, nz)), dma((2, nz)), dma((2, nz)), dma((2, nz)),
            dma((nz,)), dma((nz,)), dma((nz,)), dma((nz,)),
            dma((2,)), dma((2,)), dma((2, nz)), dma((2, nz)), dma((2, nz)), dma((2, nz)),
            dma((nz - 1,)), dma((nz - 1,)), dma, dma,
        ],
        compiler_params=pltpu.CompilerParams(
            collective_id=0, has_side_effects=True, vmem_limit_bytes=60 * 1024 * 1024
        ),
    )(tokens, gate_weights.T, expert_ids.T, w_gate, w_up, w_down)


def local(tokens, gate_weights, expert_ids, w_gate, w_up, w_down):
    tok_dev, half = tokens.shape
    devices, cores = lax.axis_size("ep"), lax.axis_size("half")
    experts = w_gate.shape[0] * devices
    gathered = tok_dev * devices * half * 2
    fits = gathered <= 8 * 1024 * 1024 and experts <= 64 and w_gate.shape[0] == 1
    shaped = cores == 2 and devices % 4 == 0 and devices > 4 and devices & (devices - 1) == 0 and tok_dev % 32 == 0
    plan = multicast if fits and shaped else slots
    return plan(tokens, gate_weights, expert_ids, w_gate, w_up, w_down)


def solution(mesh):
    placed = (
        P("ep", "half"),
        P("ep", None),
        P("ep", None),
        P("ep", None, "half"),
        P("ep", None, "half"),
        P("ep", "half", None),
    )
    return jax.shard_map(
        local, mesh=mesh, in_specs=placed, out_specs=P("ep", "half"), check_vma=False
    )
```

profile of v0, /device:TPU:0, one launch (start us, length us, event | category | flops | bytes accessed | tf_op | source)
XLA Modules:
  0.0 96.0 jit_solution(17392221476247306335)
XLA Ops:
  0.0 94.4 %shard_map.64 = bf16[128,1024]{1,0:T(8,128)(2,1)} custom-call(bf16[128,1024]{1,0:T(8,128)(2,1)} %tok_ref.1, f32[8,128]{1,0:T(8,128)} %bitcast.2, s32[8,128]{1,0:T(8,128)} %bitcast.3, bf16[1,2048,384]{2,1,0:T(8,128)(2,1)} %wg_ref.1, bf16[1,2048,384]{2,1,0:T(8,128)(2,1)} %wu_ref.1, bf16[1,384,2048]{2,1,0:T(8,128)(2,1)} %wd_ref.1), custom_call_target="tpu_custom_call" | custom-call | tf_op jit(solution)/shard_map/pallas_call | solution.py:264
  94.4 1.7 %copy.8 = bf16[128,1024]{1,0:T(8,128)(2,1)} copy(bf16[128,1024]{1,0:T(8,128)(2,1)} %shard_map.64) | data formatting | bytes 524288
where the time goes:
time: 96.2 us; the launch traced here: 96 us
  Pallas kernels  94.4 us (98%)
  local copies, waits for them, and re-layouts  1.67 us (2%)
    pallas_call x1, Pallas kernels, multicast(): pl.pallas_call(functools.partial(kernel, nz), out_shape=jax.ShapeDtypeStr...  94.4 us

commit v1 on v0

v1 whole, which is shorter than its diff:
```python
import functools

import jax
import jax.numpy as jnp
from jax import lax
from jax.experimental import pallas as pl
from jax.experimental.pallas import tpu as pltpu
from jax.sharding import PartitionSpec as P

MESH = pl.DeviceIdType.MESH


def slot_count(tok_dev, top, experts):
    return min(tok_dev, max(2, 5 * tok_dev * top // (4 * experts)))


def slots(tokens, gate_weights, expert_ids, w_gate, w_up, w_down):
    tok_dev, half_width = tokens.shape
    top = expert_ids.shape[1]
    local_experts = w_gate.shape[0]
    experts = local_experts * lax.axis_size("ep")
    capacity = slot_count(tok_dev, top, experts)
    flat_ids = expert_ids.reshape(-1)
    columns = jnp.arange(experts, dtype=jnp.int32)
    onehot = (flat_ids[:, None] == columns[None, :]).astype(jnp.int32)
    ranks = jnp.sum((jnp.cumsum(onehot, axis=0) - onehot) * onehot, axis=1)
    slot = flat_ids * capacity + ranks
    token_of_pair = jnp.arange(tok_dev * top, dtype=jnp.int32) // top
    token_table = jnp.zeros((experts * capacity,), jnp.int32).at[slot].set(token_of_pair)
    filled = (
        jnp.zeros((experts * capacity,), jnp.bfloat16)
        .at[slot]
        .set(jnp.ones((tok_dev * top,), jnp.bfloat16))
    )
    outgoing = (tokens[token_table] * filled[:, None]).reshape(experts, capacity, half_width)
    received = lax.all_to_all(outgoing, "ep", split_axis=0, concat_axis=0, tiled=True)
    count = received.shape[1]
    whole = lax.all_gather(received, "half", axis=2, tiled=True)
    width = whole.shape[2]
    grouped = whole.reshape(-1, local_experts, count, width)
    gate = jnp.einsum("secd,edf->secf", grouped, w_gate, preferred_element_type=jnp.float32)
    up = jnp.einsum("secd,edf->secf", grouped, w_up, preferred_element_type=jnp.float32)
    hidden = (jax.nn.silu(gate) * up).astype(jnp.bfloat16)
    partial_out = jnp.einsum("secf,efd->secd", hidden, w_down, preferred_element_type=jnp.float32)
    partial_out = partial_out.astype(jnp.bfloat16).reshape(experts, count, width)
    widened = lax.optimization_barrier(partial_out).astype(jnp.float32)
    summed = lax.psum_scatter(widened.astype(jnp.bfloat16), "half", scatter_dimension=2, tiled=True)
    answer = lax.all_to_all(summed, "ep", split_axis=0, concat_axis=0, tiled=True)
    picked = answer.reshape(experts * capacity, -1)[slot].reshape(tok_dev, top, -1)
    slot_out = picked.astype(jnp.float32)
    mixed = jnp.einsum("tk,tkx->tx", gate_weights, slot_out)
    return mixed.astype(jnp.bfloat16)


def kernel(cap, tok_ref, gw_ref, ids_ref, wg_ref, wu_ref, wd_ref, out_ref,
           xo, xa, yb, rows_in, cx, cy, rx, ry, tab, wgu, wdn, po, pin, mine, res,
           rda, rdb, rcx, rcy, fx, fy, rfx, rfy, zs, zin, own, load_sem, ssem, rsem):
    ep = lax.axis_index("ep")
    core = lax.axis_index("half")
    x, y, z = ep % 2, (ep // 2) % 2, ep // 4
    tok, half = out_ref.shape
    part, ff = half // 2, wg_ref.shape[2]
    experts = tab.shape[2] // 2
    nz = tab.shape[0]
    f32, bf = jnp.float32, jnp.bfloat16
    inner = ((z + 1) // 2) % 2
    ex, ey = z * 4 + y * 2 + (1 - x), z * 4 + (1 - y) * 2 + x
    other, xn, yn = {"half": 1 - core}, {"ep": ex}, {"ep": ey}
    z1 = {"ep": (z + 1 - 2 * (z % 2)) * 4 + y * 2 + x}
    z3 = {"ep": (nz - 1 - z) * 4 + y * 2 + x}
    left, right = pl.ds(0, part), pl.ds(part, part)
    names = {}

    def send(name, src, dst, to):
        at = names.setdefault(name, len(names))
        return pltpu.make_async_remote_copy(
            src_ref=src, dst_ref=dst, send_sem=ssem.at[at], recv_sem=rsem.at[at],
            device_id=to, device_id_type=MESH,
        )

    sent = []

    def go(*args):
        copy = send(*args)
        copy.start()
        sent.append(copy)
        return copy

    h0, h1 = pl.ds(core * half, half), pl.ds((1 - core) * half, half)
    loads = []
    for at, (src, cols) in enumerate(((wg_ref, pl.ds(0, ff)), (wu_ref, pl.ds(ff, ff)))):
        for side, rows in enumerate((h0, h1)):
            loads.append(pltpu.make_async_copy(
                src.at[0, rows], wgu.at[pl.ds(side * half, half), cols], load_sem.at[2 * at + side]))
    for side, cols in enumerate((h0, h1)):
        cols = pl.ds(pl.multiple_of(cols.start, 128), half)
        loads.append(pltpu.make_async_copy(
            wd_ref.at[0, :, cols], wdn.at[:, pl.ds(side * half, half)], load_sem.at[4 + side]))
    for load in loads:
        load.start()

    expert_at = lax.broadcasted_iota(jnp.int32, (experts, tok), 0)
    chosen, weight = jnp.zeros((experts, tok), f32), jnp.zeros((experts, tok), f32)
    for k in range(ids_ref.shape[0]):
        hit = expert_at == ids_ref[k : k + 1, :]
        chosen += jnp.where(hit, 1.0, 0.0)
        weight += jnp.where(hit, gw_ref[k : k + 1, :], 0.0)
    before = lax.broadcasted_iota(jnp.int32, (tok, tok), 0) < lax.broadcasted_iota(jnp.int32, (tok, tok), 1)
    rank = jnp.dot(chosen.astype(bf), jnp.where(before, 1.0, 0.0).astype(bf), preferred_element_type=f32)
    tab[0, 0, 0:experts] = jnp.where(chosen > 0.0, rank, -1.0).astype(bf)
    tab[0, 0, experts : 2 * experts] = weight.astype(bf)

    barrier = pltpu.get_barrier_semaphore()
    for partner in (other, xn, yn, z1):
        pl.semaphore_signal(barrier, inc=1, device_id=partner, device_id_type=MESH)

    @pl.when(inner == 1)
    def _():
        pl.semaphore_signal(barrier, inc=1, device_id=z3, device_id_type=MESH)

    pl.semaphore_wait(barrier, 4 + inner)

    def block(d):
        return tok_ref if d == 0 else xo.at[d - 1]

    def piece(d, p):
        if p == 2:
            return tab.at[d, 0]
        return block(d).at[:, left if p == 0 else right]

    def along(d, p, came, to):
        return send(("z", d, p), piece(came, p), piece(d, p), to)

    order = (2, 0, 1)
    for p in order:
        along(1, p, 0, z1).start()

        @pl.when(inner == 1)
        def _():
            along(3, p, 0, z3).start()

        if p == 0:
            go(("xf", 0), piece(0, 0), xa.at[0], xn)
        if p == 1:
            go(("yf", 0), piece(0, 1), yb.at[0], yn)
        if p == 2:
            go(("xt", 0), tab.at[0, 0], tab.at[0, 1], xn)
            go(("yt", 0), tab.at[0, 0], tab.at[0, 2], yn)

    slot_at = lax.broadcasted_iota(jnp.int32, (cap, tok), 0).astype(f32)

    def row(d, line, e, base):
        table = tab[d, line, base : base + experts].astype(f32)
        return jnp.sum(jnp.where(expert_at == e, table, 0.0), axis=0, keepdims=True)

    def pick(d, line, es):
        parts = [jnp.where(slot_at == row(d, line, e, 0), 1.0, 0.0).astype(bf) for e in es]
        return jnp.concatenate(parts, axis=0)

    def spread(d, line, e, values):
        w = jnp.where(slot_at == row(d, line, e, 0), row(d, line, e, experts), 0.0)
        return lax.dot_general(w.astype(bf), values, (((0,), (0,)), ((), ())), preferred_element_type=f32)

    def waits(*copies):
        for copy in copies:
            copy.wait_recv()

    def expect(name, ref):
        send(name, ref, ref, other).wait_recv()

    def arrive(d):
        for p in order:
            if d == 3:
                @pl.when(inner == 0)
                def _():
                    expect(("z", 3, p), piece(3, p))
            else:
                expect(("z", d, p), piece(d, p))

            @pl.when(inner == 1)
            def _():
                if d == 1:
                    along(2, p, 1, z3).start()
                    expect(("z", 3, p), piece(3, p))
                    pltpu.make_async_remote_copy(
                        src_ref=piece(3, p), dst_ref=piece(2, p),
                        send_sem=ssem.at[names.setdefault(("z2", p), len(names))], recv_sem=rsem.at[names[("z", 2, p)]],
                        device_id=z1, device_id_type=MESH).start()
                if d == 2:
                    pltpu.make_async_remote_copy(
                        src_ref=piece(2, p), dst_ref=piece(3, p),
                        send_sem=ssem.at[names.setdefault(("z3", p), len(names))],
                        recv_sem=rsem.at[names[("z", 3, p)]],
                        device_id=z1, device_id_type=MESH).start()

            if p == 0:
                go(("xf", d), piece(d, 0), xa.at[d], xn)
            if p == 1:
                go(("yf", d), piece(d, 1), yb.at[d], yn)
            if p == 2:
                go(("xt", d), tab.at[d, 0], tab.at[d, 1], xn)
                go(("yt", d), tab.at[d, 0], tab.at[d, 2], yn)

    c1, c2, c3, c4 = (pl.ds(i * cap, cap) for i in range(4))
    lo, hi = pl.ds(0, half), pl.ds(half, half)

    def first(d):
        got = jnp.dot(pick(d, 0, (ep, ey)), block(d)[:, left], preferred_element_type=f32).astype(bf)
        rows_in[d, c1, left] = got[:cap]
        cy[d] = got[cap:]
        go(("yc", d), cy.at[d], rows_in.at[d, c3, left], yn)
        got = jnp.dot(pick(d, 0, (ep, ex)), block(d)[:, right], preferred_element_type=f32).astype(bf)
        rows_in[d, c1, right] = got[:cap]
        cx[d] = got[cap:]
        go(("xc", d), cx.at[d], rows_in.at[d, c2, right], xn)
        go(("g1", d), rows_in.at[d, c1, lo], rows_in.at[d, c1, hi], other)

    def second(d):
        expect(("xt", d), tab.at[d, 1])
        expect(("xf", d), xa.at[d])
        got = jnp.dot(pick(d, 1, (ep, ey)), xa[d], preferred_element_type=f32).astype(bf)
        rows_in[d, c2, left] = got[:cap]
        ry[d] = got[cap:]
        go(("yr", d), ry.at[d], rows_in.at[d, c4, left], yn)
        expect(("yt", d), tab.at[d, 2])
        expect(("yf", d), yb.at[d])
        got = jnp.dot(pick(d, 2, (ep, ex)), yb[d], preferred_element_type=f32).astype(bf)
        rows_in[d, c3, right] = got[:cap]
        rx[d] = got[cap:]
        go(("xr", d), rx.at[d], rows_in.at[d, c4, right], xn)

    mid = pl.ds(cap, 2 * cap)

    def third(d):
        expect(("xc", d), rows_in.at[d, c2, right])
        expect(("yc", d), rows_in.at[d, c3, left])
        go(("g2", d), rows_in.at[d, mid, lo], rows_in.at[d, mid, hi], other)
        expect(("yr", d), rows_in.at[d, c4, left])
        expect(("xr", d), rows_in.at[d, c4, right])
        go(("g3", d), rows_in.at[d, c4, lo], rows_in.at[d, c4, hi], other)

    def compute(d):
        expect(("g1", d), rows_in.at[d, c1, hi])
        expect(("g2", d), rows_in.at[d, mid, hi])
        expect(("g3", d), rows_in.at[d, c4, hi])
        gu = jnp.dot(rows_in[d], wgu[...], preferred_element_type=f32)
        gate, up = gu[:, :ff], gu[:, ff:]
        hidden = (gate / (1.0 + jnp.exp(-gate)) * up).astype(bf)
        po[d] = jnp.dot(hidden, wdn[:, half:], preferred_element_type=f32).astype(bf)
        go(("p", d), po.at[d], pin.at[d], other)
        mine[d] = jnp.dot(hidden, wdn[:, :half], preferred_element_type=f32).astype(bf)

    def close(d):
        expect(("p", d), pin.at[d])
        res[d] = (mine[d].astype(f32) + pin[d].astype(f32)).astype(bf)
        go(("da", d), res.at[d, c4, left], rda.at[d], yn)
        go(("db", d), res.at[d, c4, right], rdb.at[d], xn)
        go(("cy", d), res.at[d, c3, left], rcy.at[d], yn)
        go(("cx", d), res.at[d, c2, right], rcx.at[d], xn)

    def relay(d):
        expect(("da", d), rda.at[d])
        fx[d] = (spread(d, 1, ep, res[d, c2, left]) + spread(d, 1, ey, rda[d])).astype(bf)
        go(("fx", d), fx.at[d], rfx.at[d], xn)
        expect(("db", d), rdb.at[d])
        fy[d] = (spread(d, 2, ep, res[d, c3, right]) + spread(d, 2, ex, rdb[d])).astype(bf)
        go(("fy", d), fy.at[d], rfy.at[d], yn)

    def home(d):
        expect(("cy", d), rcy.at[d])
        expect(("fx", d), rfx.at[d])
        a = spread(d, 0, ep, res[d, c1, left]) + spread(d, 0, ey, rcy[d]) + rfx[d].astype(f32)
        expect(("cx", d), rcx.at[d])
        expect(("fy", d), rfy.at[d])
        b = spread(d, 0, ep, res[d, c1, right]) + spread(d, 0, ex, rcx[d]) + rfy[d].astype(f32)
        if d:
            zs[d - 1, :, left] = a.astype(bf)
            zs[d - 1, :, right] = b.astype(bf)

            @pl.when(inner == 0)
            def _():
                send(("s", d), zs.at[d - 1], zin.at[d - 1], z1).start()
        else:
            own[:, left] = a
            own[:, right] = b

    def link(got, add, name, to, slot):
        expect(got, zin.at[0])
        at = got[1] - 1
        zs[add - 1] = (zs[add - 1].astype(f32) + zin[at].astype(f32)).astype(bf)
        send(name, zs.at[add - 1], zin.at[slot], to).start()

    arrive0 = [first, second]
    for stage in arrive0:
        stage(0)
    arrive(1)
    first(1)
    third(0)
    second(1)
    for load in loads:
        load.wait()
    compute(0)
    arrive(2)
    first(2)
    third(1)
    second(2)
    compute(1)
    arrive(3)
    first(3)
    third(2)
    second(3)
    compute(2)
    close(2)
    close(1)
    third(3)
    compute(3)
    close(3)
    relay(2)
    relay(3)
    close(0)
    relay(1)
    home(2)
    home(3)

    @pl.when(inner == 1)
    def _():
        link(("s", 2), 3, ("s", 4), z3, 3)
        link(("s", 3), 2, ("s", 5), z3, 4)

    relay(0)
    home(1)

    @pl.when(inner == 1)
    def _():
        link(("s", 5), 1, ("s", 6), z1, 5)

    home(0)

    @pl.when(inner == 1)
    def _():
        expect(("s", 1), zin.at[0])
        expect(("s", 4), zin.at[3])
        total = own[...] + zin[0].astype(f32) + zin[3].astype(f32)
        out_ref[...] = total.astype(bf)
        for copy in (
            [send(("z", 3, p), piece(0, p), piece(3, p), z3) for p in order]
            + [send(("z", 2, p), piece(1, p), piece(2, p), z3) for p in order]
            + [send(("z2", p), piece(3, p), piece(2, p), z1) for p in order]
            + [send(("z3", p), piece(2, p), piece(3, p), z1) for p in order]
            + [send(("s", 4 + i), zs.at[0], zin.at[0], z3) for i in range(3)]
        ):
            copy.wait_send()

    @pl.when(inner == 0)
    def _():
        expect(("s", 6), zin.at[5])
        out_ref[...] = (own[...] + zin[5].astype(f32)).astype(bf)
        for d in range(1, nz):
            send(("s", d), zs.at[d - 1], zin.at[d - 1], z1).wait_send()

    for p in order:
        along(1, p, 0, z1).wait_send()
    for copy in sent:
        copy.wait_send()


def multicast(tokens, gate_weights, expert_ids, w_gate, w_up, w_down):
    tok, half = tokens.shape
    experts = w_gate.shape[0] * lax.axis_size("ep")
    nz = lax.axis_size("ep") // 4
    part, width, ff = half // 2, w_gate.shape[1], w_gate.shape[2]
    cap = slot_count(tok, expert_ids.shape[1], experts)
    bf, dma = jnp.bfloat16, pltpu.SemaphoreType.DMA
    vmem, hbm = pl.BlockSpec(memory_space=pltpu.VMEM), pl.BlockSpec(memory_space=pl.ANY)
    compact, full = pltpu.VMEM((nz, cap, part), bf), pltpu.VMEM((nz, tok, part), bf)
    wide = pltpu.VMEM((nz, 4 * cap, half), bf)
    return pl.pallas_call(
        functools.partial(kernel, cap),
        out_shape=jax.ShapeDtypeStruct((tok, half), bf),
        in_specs=[vmem, vmem, vmem, hbm, hbm, hbm],
        out_specs=vmem,
        scratch_shapes=[
            pltpu.VMEM((nz - 1, tok, half), bf), full, full,
            pltpu.VMEM((nz, 4 * cap, width), bf),
            compact, compact, compact, compact,
            pltpu.VMEM((nz, 3, 2 * experts, tok), bf),
            pltpu.VMEM((width, 2 * ff), bf),
            pltpu.VMEM((ff, width), bf),
            wide, wide, wide, wide,
            compact, compact, compact, compact,
            full, full, full, full,
            pltpu.VMEM((nz - 1, tok, half), bf),
            pltpu.VMEM((6, tok, half), bf),
            pltpu.VMEM((tok, half), jnp.float32),
            dma((6,)), dma((104,)), dma((104,)),
        ],
        compiler_params=pltpu.CompilerParams(
            collective_id=0, has_side_effects=True, vmem_limit_bytes=60 * 1024 * 1024
        ),
    )(tokens, gate_weights.T, expert_ids.T, w_gate, w_up, w_down)


def local(tokens, gate_weights, expert_ids, w_gate, w_up, w_down):
    tok_dev, half = tokens.shape
    devices, cores = lax.axis_size("ep"), lax.axis_size("half")
    experts = w_gate.shape[0] * devices
    cap = slot_count(tok_dev, expert_ids.shape[1], experts)
    fits = tok_dev * devices * half * 2 <= 8 * 1024 * 1024 and w_gate.shape[0] == 1
    shaped = cores == 2 and devices == 4 * 4 and tok_dev == 128
    tiled = cap % 16 == 0 and half % 256 == 0 and experts % 16 == 0 and w_gate.shape[2] % 128 == 0
    plan = multicast if fits and shaped and tiled else slots
    return plan(tokens, gate_weights, expert_ids, w_gate, w_up, w_down)


def solution(mesh):
    placed = (
        P("ep", "half"),
        P("ep", None),
        P("ep", None),
        P("ep", None, "half"),
        P("ep", None, "half"),
        P("ep", "half", None),
    )
    return jax.shard_map(
        local, mesh=mesh, in_specs=placed, out_specs=P("ep", "half"), check_vma=False
    )
```

time: 96.2 us -> 86.3 us (0.90)
  Pallas kernels: 94.4 us -> 83.5 us
    pallas_call x1, Pallas kernels: 94.4 us -> 83.5 us  [multicast(): pl.pallas_call(functools.partial(kernel, cap), out_shape=jax.ShapeDtypeSt...]
where the time goes in v1:
time: 86.3 us; the launch traced here: 85.2 us
  Pallas kernels  83.5 us (97%)
  local copies, waits for them, and re-layouts  1.67 us (2%)
    pallas_call x1, Pallas kernels, multicast(): pl.pallas_call(functools.partial(kernel, cap), out_shape=jax.ShapeDtypeSt...  83.5 us

profile of v1, /device:TPU:0, one launch (start us, length us, event | category | flops | bytes accessed | tf_op | source)
XLA Modules:
  0.0 85.2 jit_solution(7911578797595171610)
XLA Ops:
  0.0 83.5 %shard_map.64 = bf16[128,1024]{1,0:T(8,128)(2,1)} custom-call(bf16[128,1024]{1,0:T(8,128)(2,1)} %tok_ref.1, f32[8,128]{1,0:T(8,128)} %bitcast.2, s32[8,128]{1,0:T(8,128)} %bitcast.3, bf16[1,2048,384]{2,1,0:T(8,128)(2,1)} %wg_ref.1, bf16[1,2048,384]{2,1,0:T(8,128)(2,1)} %wu_ref.1, bf16[1,384,2048]{2,1,0:T(8,128)(2,1)} %wd_ref.1), custom_call_target="tpu_custom_call" | custom-call | tf_op jit(solution)/shard_map/pallas_call | solution.py:377
  83.5 1.7 %copy.8 = bf16[128,1024]{1,0:T(8,128)(2,1)} copy(bf16[128,1024]{1,0:T(8,128)(2,1)} %shard_map.64) | data formatting | bytes 524288

commit v2 on v1

--- a/solution.py
+++ b/solution.py
@@ -52,6 +52,14 @@
     return mixed.astype(jnp.bfloat16)
 
 
+PLANS = (
+    "F0 A12 A10 S0 A11 F1 A22 A20 T0 S1 W C0 A21 F2 A32 T1 A30 S2 A31 F3 C1 K0 T2 S3 C2 K1"
+    " T3 K2 R1 C3 R2 H1 K3 H2 R3 R0 H3 H0",
+    "F0 A12 A22 A10 A20 S0 A11 A21 F1 F2 A32 A30 T0 S1 A31 F3 W C0 S2 T1 C1 K0 T2 S3 C2 K1"
+    " T3 K2 R1 C3 R2 H1 K3 H2 R3 R0 H3 H0",
+)
+
+
 def kernel(cap, tok_ref, gw_ref, ids_ref, wg_ref, wu_ref, wd_ref, out_ref,
            xo, xa, yb, rows_in, cx, cy, rx, ry, tab, wgu, wdn, po, pin, mine, res,
            rda, rdb, rcx, rcy, fx, fy, rfx, rfy, zs, zin, own, load_sem, ssem, rsem):
@@ -59,7 +67,7 @@
     core = lax.axis_index("half")
     x, y, z = ep % 2, (ep // 2) % 2, ep // 4
     tok, half = out_ref.shape
-    part, ff = half // 2, wg_ref.shape[2]
+    part, rows, ff = half // 2, tok // 2, wg_ref.shape[2]
     experts = tab.shape[2] // 2
     nz = tab.shape[0]
     f32, bf = jnp.float32, jnp.bfloat16
@@ -71,27 +79,29 @@
     left, right = pl.ds(0, part), pl.ds(part, part)
     names = {}
 
-    def send(name, src, dst, to):
+    def send(name, src, dst, to, lands=None):
         at = names.setdefault(name, len(names))
+        got = at if lands is None else names.setdefault(lands, len(names))
         return pltpu.make_async_remote_copy(
-            src_ref=src, dst_ref=dst, send_sem=ssem.at[at], recv_sem=rsem.at[at],
+            src_ref=src, dst_ref=dst, send_sem=ssem.at[at], recv_sem=rsem.at[got],
             device_id=to, device_id_type=MESH,
         )
 
     sent = []
 
-    def go(*args):
-        copy = send(*args)
+    def move(copy):
         copy.start()
         sent.append(copy)
-        return copy
+
+    def go(*args):
+        move(send(*args))
 
     h0, h1 = pl.ds(core * half, half), pl.ds((1 - core) * half, half)
     loads = []
     for at, (src, cols) in enumerate(((wg_ref, pl.ds(0, ff)), (wu_ref, pl.ds(ff, ff)))):
-        for side, rows in enumerate((h0, h1)):
+        for side, deep in enumerate((h0, h1)):
             loads.append(pltpu.make_async_copy(
-                src.at[0, rows], wgu.at[pl.ds(side * half, half), cols], load_sem.at[2 * at + side]))
+                src.at[0, deep], wgu.at[pl.ds(side * half, half), cols], load_sem.at[2 * at + side]))
     for side, cols in enumerate((h0, h1)):
         cols = pl.ds(pl.multiple_of(cols.start, 128), half)
         loads.append(pltpu.make_async_copy(
@@ -124,28 +134,28 @@
         return tok_ref if d == 0 else xo.at[d - 1]
 
     def piece(d, p):
+        return tab.at[d, 0] if p == 2 else block(d).at[pl.ds(p * rows, rows)]
+
+    def hop(name, lands, p, came, to):
+        return send((name, p), piece(came, p), piece(lands, p), to, ("z", lands, p))
+
+    def plane(d, p):
         if p == 2:
-            return tab.at[d, 0]
-        return block(d).at[:, left if p == 0 else right]
-
-    def along(d, p, came, to):
-        return send(("z", d, p), piece(came, p), piece(d, p), to)
+            go(("xt", d), tab.at[d, 0], tab.at[d, 1], xn)
+            go(("yt", d), tab.at[d, 0], tab.at[d, 2], yn)
+        else:
+            here = pl.ds(p * rows, rows)
+            go(("xf", d, p), block(d).at[here, left], xa.at[d, here], xn)
+            go(("yf", d, p), block(d).at[here, right], yb.at[d, here], yn)
 
     order = (2, 0, 1)
-    for p in order:
-        along(1, p, 0, z1).start()
-
-        @pl.when(inner == 1)
-        def _():
-            along(3, p, 0, z3).start()
-
-        if p == 0:
-            go(("xf", 0), piece(0, 0), xa.at[0], xn)
-        if p == 1:
-            go(("yf", 0), piece(0, 1), yb.at[0], yn)
-        if p == 2:
-            go(("xt", 0), tab.at[0, 0], tab.at[0, 1], xn)
-            go(("yt", 0), tab.at[0, 0], tab.at[0, 2], yn)
+
+    def begin(role):
+        for p in order:
+            move(hop("z own", 1 if role else 2, p, 0, z1))
+            if role:
+                move(hop("z far", 1, p, 0, z3))
+            plane(0, p)
 
     slot_at = lax.broadcasted_iota(jnp.int32, (cap, tok), 0).astype(f32)
 
@@ -161,45 +171,15 @@
         w = jnp.where(slot_at == row(d, line, e, 0), row(d, line, e, experts), 0.0)
         return lax.dot_general(w.astype(bf), values, (((0,), (0,)), ((), ())), preferred_element_type=f32)
 
-    def waits(*copies):
-        for copy in copies:
-            copy.wait_recv()
-
     def expect(name, ref):
         send(name, ref, ref, other).wait_recv()
 
-    def arrive(d):
-        for p in order:
-            if d == 3:
-                @pl.when(inner == 0)
-                def _():
-                    expect(("z", 3, p), piece(3, p))
-            else:
-                expect(("z", d, p), piece(d, p))
-
-            @pl.when(inner == 1)
-            def _():
-                if d == 1:
-                    along(2, p, 1, z3).start()
-                    expect(("z", 3, p), piece(3, p))
-                    pltpu.make_async_remote_copy(
-                        src_ref=piece(3, p), dst_ref=piece(2, p),
-                        send_sem=ssem.at[names.setdefault(("z2", p), len(names))], recv_sem=rsem.at[names[("z", 2, p)]],
-                        device_id=z1, device_id_type=MESH).start()
-                if d == 2:
-                    pltpu.make_async_remote_copy(
-                        src_ref=piece(2, p), dst_ref=piece(3, p),
-                        send_sem=ssem.at[names.setdefault(("z3", p), len(names))],
-                        recv_sem=rsem.at[names[("z", 3, p)]],
-                        device_id=z1, device_id_type=MESH).start()
-
-            if p == 0:
-                go(("xf", d), piece(d, 0), xa.at[d], xn)
-            if p == 1:
-                go(("yf", d), piece(d, 1), yb.at[d], yn)
-            if p == 2:
-                go(("xt", d), tab.at[d, 0], tab.at[d, 1], xn)
-                go(("yt", d), tab.at[d, 0], tab.at[d, 2], yn)
+    def arrive(role, d, p):
+        expect(("z", d, p), piece(d, p))
+        if role:
+            lands, to = ((2, z1), (3, z3), (3, z1))[d - 1]
+            move(hop("z on" + str(d), lands, p, d, to))
+        plane(d, p)
 
     c1, c2, c3, c4 = (pl.ds(i * cap, cap) for i in range(4))
     lo, hi = pl.ds(0, half), pl.ds(half, half)
@@ -217,13 +197,15 @@
 
     def second(d):
         expect(("xt", d), tab.at[d, 1])
-        expect(("xf", d), xa.at[d])
+        for p in range(2):
+            expect(("xf", d, p), xa.at[d, pl.ds(p * rows, rows)])
         got = jnp.dot(pick(d, 1, (ep, ey)), xa[d], preferred_element_type=f32).astype(bf)
         rows_in[d, c2, left] = got[:cap]
         ry[d] = got[cap:]
         go(("yr", d), ry.at[d], rows_in.at[d, c4, left], yn)
         expect(("yt", d), tab.at[d, 2])
-        expect(("yf", d), yb.at[d])
+        for p in range(2):
+            expect(("yf", d, p), yb.at[d, pl.ds(p * rows, rows)])
         got = jnp.dot(pick(d, 2, (ep, ex)), yb[d], preferred_element_type=f32).astype(bf)
         rows_in[d, c3, right] = got[:cap]
         rx[d] = got[cap:]
@@ -266,102 +248,50 @@
         fy[d] = (spread(d, 2, ep, res[d, c3, right]) + spread(d, 2, ex, rdb[d])).astype(bf)
         go(("fy", d), fy.at[d], rfy.at[d], yn)
 
-    def home(d):
-        expect(("cy", d), rcy.at[d])
-        expect(("fx", d), rfx.at[d])
-        a = spread(d, 0, ep, res[d, c1, left]) + spread(d, 0, ey, rcy[d]) + rfx[d].astype(f32)
-        expect(("cx", d), rcx.at[d])
-        expect(("fy", d), rfy.at[d])
-        b = spread(d, 0, ep, res[d, c1, right]) + spread(d, 0, ex, rcx[d]) + rfy[d].astype(f32)
-        if d:
-            zs[d - 1, :, left] = a.astype(bf)
-            zs[d - 1, :, right] = b.astype(bf)
-
-            @pl.when(inner == 0)
-            def _():
-                send(("s", d), zs.at[d - 1], zin.at[d - 1], z1).start()
-        else:
-            own[:, left] = a
-            own[:, right] = b
-
-    def link(got, add, name, to, slot):
-        expect(got, zin.at[0])
-        at = got[1] - 1
-        zs[add - 1] = (zs[add - 1].astype(f32) + zin[at].astype(f32)).astype(bf)
-        send(name, zs.at[add - 1], zin.at[slot], to).start()
-
-    arrive0 = [first, second]
-    for stage in arrive0:
-        stage(0)
-    arrive(1)
-    first(1)
-    third(0)
-    second(1)
-    for load in loads:
-        load.wait()
-    compute(0)
-    arrive(2)
-    first(2)
-    third(1)
-    second(2)
-    compute(1)
-    arrive(3)
-    first(3)
-    third(2)
-    second(3)
-    compute(2)
-    close(2)
-    close(1)
-    third(3)
-    compute(3)
-    close(3)
-    relay(2)
-    relay(3)
-    close(0)
-    relay(1)
-    home(2)
-    home(3)
-
-    @pl.when(inner == 1)
-    def _():
-        link(("s", 2), 3, ("s", 4), z3, 3)
-        link(("s", 3), 2, ("s", 5), z3, 4)
-
-    relay(0)
-    home(1)
-
-    @pl.when(inner == 1)
-    def _():
-        link(("s", 5), 1, ("s", 6), z1, 5)
-
-    home(0)
-
-    @pl.when(inner == 1)
-    def _():
-        expect(("s", 1), zin.at[0])
-        expect(("s", 4), zin.at[3])
-        total = own[...] + zin[0].astype(f32) + zin[3].astype(f32)
-        out_ref[...] = total.astype(bf)
-        for copy in (
-            [send(("z", 3, p), piece(0, p), piece(3, p), z3) for p in order]
-            + [send(("z", 2, p), piece(1, p), piece(2, p), z3) for p in order]
-            + [send(("z2", p), piece(3, p), piece(2, p), z1) for p in order]
-            + [send(("z3", p), piece(2, p), piece(3, p), z1) for p in order]
-            + [send(("s", 4 + i), zs.at[0], zin.at[0], z3) for i in range(3)]
-        ):
+    apart = (z + 1 - 2 * (z % 2), (z + 2) % nz, nz - 1 - z)
+    def home(role, d):
+        for p, cols in enumerate((left, right)):
+            e, part_in, full = (ey, rcy, rfx) if p == 0 else (ex, rcx, rfy)
+            expect(("cy" if p == 0 else "cx", d), part_in.at[d])
+            expect(("fx" if p == 0 else "fy", d), full.at[d])
+            total = spread(d, 0, ep, res[d, c1, cols]) + spread(d, 0, e, part_in[d]) + full[d].astype(f32)
+            if d == 0:
+                own[:, cols] = total
+                continue
+            zs[d - 1, :, cols] = total.astype(bf)
+            step = (d + 1) % 3 if role else d - 1
+            go(("o", d, p), zs.at[d - 1, :, cols], zin.at[step, :, cols],
+               {"ep": apart[step] * 4 + y * 2 + x}, ("s", step, p))
+
+    def ready(_):
+        for load in loads:
+            load.wait()
+
+    def finish(_):
+        for p, cols in enumerate((left, right)):
+            total = own[:, cols]
+            for d in range(nz - 1):
+                expect(("s", d, p), zin.at[d, :, cols])
+                total += zin[d, :, cols].astype(f32)
+            out_ref[:, cols] = total.astype(bf)
+        for copy in sent:
             copy.wait_send()
-
-    @pl.when(inner == 0)
-    def _():
-        expect(("s", 6), zin.at[5])
-        out_ref[...] = (own[...] + zin[5].astype(f32)).astype(bf)
-        for d in range(1, nz):
-            send(("s", d), zs.at[d - 1], zin.at[d - 1], z1).wait_send()
-
-    for p in order:
-        along(1, p, 0, z1).wait_send()
-    for copy in sent:
-        copy.wait_send()
+        sent.clear()
+
+    steps = {"F": first, "S": second, "T": third, "C": compute, "K": close, "R": relay}
+    for role, plan in enumerate(PLANS):
+        @pl.when(inner == role)
+        def _():
+            begin(role)
+            for word in plan.split():
+                at = [int(v) for v in word[1:]]
+                if word[0] in "AH":
+                    {"A": arrive, "H": home}[word[0]](role, *at)
+                elif word[0] == "W":
+                    ready(at)
+                else:
+                    steps[word[0]](*at)
+            finish(role)
 
 
 def multicast(tokens, gate_weights, expert_ids, w_gate, w_up, w_down):
@@ -390,9 +320,9 @@
             compact, compact, compact, compact,
             full, full, full, full,
             pltpu.VMEM((nz - 1, tok, half), bf),
-            pltpu.VMEM((6, tok, half), bf),
+            pltpu.VMEM((nz - 1, tok, half), bf),
             pltpu.VMEM((tok, half), jnp.float32),
-            dma((6,)), dma((104,)), dma((104,)),
+            dma((6,)), dma((136,)), dma((136,)),
         ],
         compiler_params=pltpu.CompilerParams(
             collective_id=0, has_side_effects=True, vmem_limit_bytes=60 * 1024 * 1024

time: 86.3 us -> 78.6 us (0.911); the launches traced: 85.2 us -> 78.4 us
  Pallas kernels: 83.5 us -> 76.7 us
    pallas_call x1, Pallas kernels: 83.5 us -> 76.7 us  [multicast(): pl.pallas_call(functools.partial(kernel, cap), out_shape=jax.ShapeDtypeSt...]
where the time goes in v2:
time: 78.6 us; the launch traced here: 78.4 us
  Pallas kernels  76.7 us (98%)
  local copies, waits for them, and re-layouts  1.67 us (2%)
    pallas_call x1, Pallas kernels, multicast(): pl.pallas_call(functools.partial(kernel, cap), out_shape=jax.ShapeDtypeSt...  76.7 us
    unnamed x1, local copies, waits for them, and re-layouts  1.67 us

profile of v2, /device:TPU:0, one launch (start us, length us, event | category | flops | bytes accessed | tf_op | source)
XLA Modules:
  0.0 78.4 jit_solution(13040268380190631881)
XLA Ops:
  0.0 76.7 %shard_map.64 = bf16[128,1024]{1,0:T(8,128)(2,1)} custom-call(bf16[128,1024]{1,0:T(8,128)(2,1)} %tok_ref.1, f32[8,128]{1,0:T(8,128)} %bitcast.2, s32[8,128]{1,0:T(8,128)} %bitcast.3, bf16[1,2048,384]{2,1,0:T(8,128)(2,1)} %wg_ref.1, bf16[1,2048,384]{2,1,0:T(8,128)(2,1)} %wu_ref.1, bf16[1,384,2048]{2,1,0:T(8,128)(2,1)} %wd_ref.1), custom_call_target="tpu_custom_call" | custom-call | tf_op jit(solution)/shard_map/pallas_call | solution.py:307
  76.7 1.7 %copy.8 = bf16[128,1024]{1,0:T(8,128)(2,1)} copy(bf16[128,1024]{1,0:T(8,128)(2,1)} %shard_map.64) | data formatting | bytes 524288

commit v3 on v2

--- a/solution.py
+++ b/solution.py
@@ -53,16 +53,29 @@
 
 
 PLANS = (
-    "F0 A12 A10 S0 A11 F1 A22 A20 T0 S1 W C0 A21 F2 A32 T1 A30 S2 A31 F3 C1 K0 T2 S3 C2 K1"
-    " T3 K2 R1 C3 R2 H1 K3 H2 R3 R0 H3 H0",
-    "F0 A12 A22 A10 A20 S0 A11 A21 F1 F2 A32 A30 T0 S1 A31 F3 W C0 S2 T1 C1 K0 T2 S3 C2 K1"
-    " T3 K2 R1 C3 R2 H1 K3 H2 R3 R0 H3 H0",
+    (
+        "A12", "X0", "F0", "A10", "W", "A11", "A22", "F1", "X1", "A20", "Y1", "T1", "A21", "A32",
+        "A30", "U1", "A31", "F3", "C1", "X3", "Y3", "K1", "X2", "Y2", "F2", "Y0", "T3", "U3", "L1",
+        "C3", "U2", "Q1", "T2", "T0", "K3", "R1", "L3", "C2", "J1", "Q3", "K2", "U0", "H1", "R3",
+        "C0", "Q2", "L2", "J3", "R2", "H3", "J2", "K0", "L0", "H2", "R0", "Q0", "H0", "J0",
+    ),
+    (
+        "A22", "F0", "A12", "A10", "A20", "A21", "A32", "A11", "A30", "F1", "Y1", "X1", "A31", "F3",
+        "T1", "X2", "U1", "Y2", "Y3", "X3", "X0", "W", "C1", "T3", "F2", "K1", "L1", "U3", "Y0",
+        "C3", "Q1", "T2", "U2", "K3", "R1", "C2", "J1", "Q3", "L3", "R3", "T0", "H1", "K2", "J3",
+        "H3", "Q2", "R2", "L2", "U0", "C0", "K0", "J2", "L0", "R0", "Q0", "H2", "H0", "J0",
+    ),
 )
 
 
-def kernel(cap, tok_ref, gw_ref, ids_ref, wg_ref, wu_ref, wd_ref, out_ref,
-           xo, xa, yb, rows_in, cx, cy, rx, ry, tab, wgu, wdn, po, pin, mine, res,
-           rda, rdb, rcx, rcy, fx, fy, rfx, rfy, zs, zin, own, load_sem, ssem, rsem):
+def kernel(cap, *refs):
+    dma = pltpu.SemaphoreType.DMA
+    pl.run_scoped(functools.partial(body, cap, *refs), dma((12,)), dma((136,)), dma((136,)))
+
+
+def body(cap, tok_hbm, gw_hbm, ids_hbm, wg_ref, wu_ref, wd_ref, out_ref,
+         tok_ref, gw_ref, ids_ref, xo, xa, yb, rows_in, cx, cy, rx, ry, tab, wgu, wdn, po, pin, mine, res,
+         rda, rdb, rcx, rcy, fx, fy, rfx, rfy, zs, zin, own, load_sem, ssem, rsem):
     ep = lax.axis_index("ep")
     core = lax.axis_index("half")
     x, y, z = ep % 2, (ep // 2) % 2, ep // 4
@@ -96,6 +109,20 @@
     def go(*args):
         move(send(*args))
 
+    barrier = pltpu.get_barrier_semaphore()
+    for partner in (other, xn, yn, z1):
+        pl.semaphore_signal(barrier, inc=1, device_id=partner, device_id_type=MESH)
+
+    @pl.when(inner == 1)
+    def _():
+        pl.semaphore_signal(barrier, inc=1, device_id=z3, device_id_type=MESH)
+
+    inputs = [
+        pltpu.make_async_copy(src, dst, load_sem.at[6 + at])
+        for at, (src, dst) in enumerate(((ids_hbm, ids_ref), (gw_hbm, gw_ref), (tok_hbm, tok_ref)))
+    ]
+    for load in inputs:
+        load.start()
     h0, h1 = pl.ds(core * half, half), pl.ds((1 - core) * half, half)
     loads = []
     for at, (src, cols) in enumerate(((wg_ref, pl.ds(0, ff)), (wu_ref, pl.ds(ff, ff)))):
@@ -109,6 +136,8 @@
     for load in loads:
         load.start()
 
+    inputs[0].wait()
+    inputs[1].wait()
     expert_at = lax.broadcasted_iota(jnp.int32, (experts, tok), 0)
     chosen, weight = jnp.zeros((experts, tok), f32), jnp.zeros((experts, tok), f32)
     for k in range(ids_ref.shape[0]):
@@ -120,14 +149,7 @@
     tab[0, 0, 0:experts] = jnp.where(chosen > 0.0, rank, -1.0).astype(bf)
     tab[0, 0, experts : 2 * experts] = weight.astype(bf)
 
-    barrier = pltpu.get_barrier_semaphore()
-    for partner in (other, xn, yn, z1):
-        pl.semaphore_signal(barrier, inc=1, device_id=partner, device_id_type=MESH)
-
-    @pl.when(inner == 1)
-    def _():
-        pl.semaphore_signal(barrier, inc=1, device_id=z3, device_id_type=MESH)
-
+    inputs[2].wait()
     pl.semaphore_wait(barrier, 4 + inner)
 
     def block(d):
@@ -195,7 +217,7 @@
         go(("xc", d), cx.at[d], rows_in.at[d, c2, right], xn)
         go(("g1", d), rows_in.at[d, c1, lo], rows_in.at[d, c1, hi], other)
 
-    def second(d):
+    def cross_x(d):
         expect(("xt", d), tab.at[d, 1])
         for p in range(2):
             expect(("xf", d, p), xa.at[d, pl.ds(p * rows, rows)])
@@ -203,6 +225,8 @@
         rows_in[d, c2, left] = got[:cap]
         ry[d] = got[cap:]
         go(("yr", d), ry.at[d], rows_in.at[d, c4, left], yn)
+
+    def cross_y(d):
         expect(("yt", d), tab.at[d, 2])
         for p in range(2):
             expect(("yf", d, p), yb.at[d, pl.ds(p * rows, rows)])
@@ -213,10 +237,12 @@
 
     mid = pl.ds(cap, 2 * cap)
 
-    def third(d):
+    def share_mid(d):
         expect(("xc", d), rows_in.at[d, c2, right])
         expect(("yc", d), rows_in.at[d, c3, left])
         go(("g2", d), rows_in.at[d, mid, lo], rows_in.at[d, mid, hi], other)
+
+    def share_far(d):
         expect(("yr", d), rows_in.at[d, c4, left])
         expect(("xr", d), rows_in.at[d, c4, right])
         go(("g3", d), rows_in.at[d, c4, lo], rows_in.at[d, c4, hi], other)
@@ -237,37 +263,41 @@
         res[d] = (mine[d].astype(f32) + pin[d].astype(f32)).astype(bf)
         go(("da", d), res.at[d, c4, left], rda.at[d], yn)
         go(("db", d), res.at[d, c4, right], rdb.at[d], xn)
+
+    def direct(d):
         go(("cy", d), res.at[d, c3, left], rcy.at[d], yn)
         go(("cx", d), res.at[d, c2, right], rcx.at[d], xn)
 
-    def relay(d):
+    def relay_x(d):
         expect(("da", d), rda.at[d])
         fx[d] = (spread(d, 1, ep, res[d, c2, left]) + spread(d, 1, ey, rda[d])).astype(bf)
         go(("fx", d), fx.at[d], rfx.at[d], xn)
+
+    def relay_y(d):
         expect(("db", d), rdb.at[d])
         fy[d] = (spread(d, 2, ep, res[d, c3, right]) + spread(d, 2, ex, rdb[d])).astype(bf)
         go(("fy", d), fy.at[d], rfy.at[d], yn)
 
     apart = (z + 1 - 2 * (z % 2), (z + 2) % nz, nz - 1 - z)
-    def home(role, d):
-        for p, cols in enumerate((left, right)):
-            e, part_in, full = (ey, rcy, rfx) if p == 0 else (ex, rcx, rfy)
-            expect(("cy" if p == 0 else "cx", d), part_in.at[d])
-            expect(("fx" if p == 0 else "fy", d), full.at[d])
-            total = spread(d, 0, ep, res[d, c1, cols]) + spread(d, 0, e, part_in[d]) + full[d].astype(f32)
-            if d == 0:
-                own[:, cols] = total
-                continue
-            zs[d - 1, :, cols] = total.astype(bf)
-            step = (d + 1) % 3 if role else d - 1
-            go(("o", d, p), zs.at[d - 1, :, cols], zin.at[step, :, cols],
-               {"ep": apart[step] * 4 + y * 2 + x}, ("s", step, p))
-
-    def ready(_):
+    def home(role, p, d):
+        cols = right if p else left
+        e, part_in, full = (ex, rcx, rfy) if p else (ey, rcy, rfx)
+        expect(("cx" if p else "cy", d), part_in.at[d])
+        expect(("fy" if p else "fx", d), full.at[d])
+        total = spread(d, 0, ep, res[d, c1, cols]) + spread(d, 0, e, part_in[d]) + full[d].astype(f32)
+        if d == 0:
+            own[:, cols] = total
+            return
+        zs[d - 1, :, cols] = total.astype(bf)
+        step = (d + 1) % 3 if role else d - 1
+        go(("o", d, p), zs.at[d - 1, :, cols], zin.at[step, :, cols],
+           {"ep": apart[step] * 4 + y * 2 + x}, ("s", step, p))
+
+    def ready():
         for load in loads:
             load.wait()
 
-    def finish(_):
+    def finish():
         for p, cols in enumerate((left, right)):
             total = own[:, cols]
             for d in range(nz - 1):
@@ -278,20 +308,26 @@
             copy.wait_send()
         sent.clear()
 
-    steps = {"F": first, "S": second, "T": third, "C": compute, "K": close, "R": relay}
+    steps = {
+        "F": first, "X": cross_x, "Y": cross_y, "T": share_mid, "U": share_far, "C": compute, "W": ready,
+        "K": close, "L": direct, "R": relay_x, "Q": relay_y,
+    }
+    def step(role, word):
+        at = [int(v) for v in word[1:]]
+        if word[0] == "A":
+            arrive(role, *at)
+        elif word[0] in "HJ":
+            home(role, "HJ".index(word[0]), *at)
+        else:
+            steps[word[0]](*at)
+
     for role, plan in enumerate(PLANS):
         @pl.when(inner == role)
         def _():
             begin(role)
-            for word in plan.split():
-                at = [int(v) for v in word[1:]]
-                if word[0] in "AH":
-                    {"A": arrive, "H": home}[word[0]](role, *at)
-                elif word[0] == "W":
-                    ready(at)
-                else:
-                    steps[word[0]](*at)
-            finish(role)
+            for word in plan:
+                step(role, word)
+            finish()
 
 
 def multicast(tokens, gate_weights, expert_ids, w_gate, w_up, w_down):
@@ -300,16 +336,19 @@
     nz = lax.axis_size("ep") // 4
     part, width, ff = half // 2, w_gate.shape[1], w_gate.shape[2]
     cap = slot_count(tok, expert_ids.shape[1], experts)
-    bf, dma = jnp.bfloat16, pltpu.SemaphoreType.DMA
+    bf = jnp.bfloat16
     vmem, hbm = pl.BlockSpec(memory_space=pltpu.VMEM), pl.BlockSpec(memory_space=pl.ANY)
     compact, full = pltpu.VMEM((nz, cap, part), bf), pltpu.VMEM((nz, tok, part), bf)
     wide = pltpu.VMEM((nz, 4 * cap, half), bf)
     return pl.pallas_call(
         functools.partial(kernel, cap),
         out_shape=jax.ShapeDtypeStruct((tok, half), bf),
-        in_specs=[vmem, vmem, vmem, hbm, hbm, hbm],
+        in_specs=[hbm] * 6,
         out_specs=vmem,
         scratch_shapes=[
+            pltpu.VMEM((tok, half), bf),
+            pltpu.VMEM((expert_ids.shape[1], tok), jnp.float32),
+            pltpu.VMEM((expert_ids.shape[1], tok), jnp.int32),
             pltpu.VMEM((nz - 1, tok, half), bf), full, full,
             pltpu.VMEM((nz, 4 * cap, width), bf),
             compact, compact, compact, compact,
@@ -322,7 +361,6 @@
             pltpu.VMEM((nz - 1, tok, half), bf),
             pltpu.VMEM((nz - 1, tok, half), bf),
             pltpu.VMEM((tok, half), jnp.float32),
-            dma((6,)), dma((136,)), dma((136,)),
         ],
         compiler_params=pltpu.CompilerParams(
             collective_id=0, has_side_effects=True, vmem_limit_bytes=60 * 1024 * 1024

time: 78.6 us -> 67.4 us (0.86)
  Pallas kernels: 76.7 us -> 65.5 us
    pallas_call x1, Pallas kernels: 76.7 us -> 65.5 us  [multicast(): pl.pallas_call(functools.partial(kernel, cap), out_shape=jax.ShapeDtypeSt...]
where the time goes in v3:
time: 67.4 us; the launch traced here: 67.2 us
  Pallas kernels  65.5 us (97%)
  local copies, waits for them, and re-layouts  1.67 us (2%)
    pallas_call x1, Pallas kernels, multicast(): pl.pallas_call(functools.partial(kernel, cap), out_shape=jax.ShapeDtypeSt...  65.5 us
    unnamed x1, local copies, waits for them, and re-layouts  1.67 us

profile of v3, /device:TPU:0, one launch (start us, length us, event | category | flops | bytes accessed | tf_op | source)
XLA Modules:
  0.0 67.2 jit_solution(6193561959502665249)
XLA Ops:
  0.0 65.5 %shard_map.64 = bf16[128,1024]{1,0:T(8,128)(2,1)} custom-call(bf16[128,1024]{1,0:T(8,128)(2,1)} %refs_0_.1, f32[8,128]{1,0:T(8,128)} %bitcast.2, s32[8,128]{1,0:T(8,128)} %bitcast.3, bf16[1,2048,384]{2,1,0:T(8,128)(2,1)} %refs_3_.1, bf16[1,2048,384]{2,1,0:T(8,128)(2,1)} %refs_4_.1, bf16[1,384,2048]{2,1,0:T(8,128)(2,1)} %refs_5_.1), custom_call_target="tpu_custom_call" | custom-call | tf_op jit(solution)/shard_map/pallas_call | solution.py:343
  65.5 1.7 %copy.8 = bf16[128,1024]{1,0:T(8,128)(2,1)} copy(bf16[128,1024]{1,0:T(8,128)(2,1)} %shard_map.64) | data formatting | bytes 524288

commit v4 on v3

--- a/solution.py
+++ b/solution.py
@@ -54,18 +54,21 @@
 
 PLANS = (
     (
-        "A12", "X0", "F0", "A10", "W", "A11", "A22", "F1", "X1", "A20", "Y1", "T1", "A21", "A32",
-        "A30", "U1", "A31", "F3", "C1", "X3", "Y3", "K1", "X2", "Y2", "F2", "Y0", "T3", "U3", "L1",
-        "C3", "U2", "Q1", "T2", "T0", "K3", "R1", "L3", "C2", "J1", "Q3", "K2", "U0", "H1", "R3",
-        "C0", "Q2", "L2", "J3", "R2", "H3", "J2", "K0", "L0", "H2", "R0", "Q0", "H0", "J0",
+        "A12", "F0", "G0", "Y0", "X0", "A10", "A11", "U0", "F1", "G1", "A22", "A20", "T0", "A21",
+        "F2", "G2", "A32", "A30", "X2", "Y2", "W", "C0", "A31", "F3", "G3", "U2", "T2", "Y3", "X3",
+        "X1", "C2", "T3", "D2", "Y1", "U3", "K2", "L2", "T1", "C3", "D3", "Q2", "K3", "R2", "U1",
+        "C1", "D1", "Q3", "L3", "J2", "K1", "R3", "H2", "D0", "J3", "Q1", "K0", "L1", "H3", "R1",
+        "J1", "Q0", "L0", "R0", "H1", "J0", "H0",
     ),
     (
-        "A22", "F0", "A12", "A10", "A20", "A21", "A32", "A11", "A30", "F1", "Y1", "X1", "A31", "F3",
-        "T1", "X2", "U1", "Y2", "Y3", "X3", "X0", "W", "C1", "T3", "F2", "K1", "L1", "U3", "Y0",
-        "C3", "Q1", "T2", "U2", "K3", "R1", "C2", "J1", "Q3", "L3", "R3", "T0", "H1", "K2", "J3",
-        "H3", "Q2", "R2", "L2", "U0", "C0", "K0", "J2", "L0", "R0", "Q0", "H2", "H0", "J0",
+        "A22", "F0", "A12", "A10", "A20", "A21", "A11", "A32", "A30", "F2", "G2", "A31", "X2", "Y2",
+        "F3", "G3", "T2", "X3", "X1", "X0", "Y3", "U2", "F1", "Y1", "G1", "G0", "T3", "W", "C2",
+        "U3", "Y0", "D2", "C3", "D3", "K2", "U1", "K3", "L3", "T1", "C1", "R3", "Q3", "U0", "R2",
+        "D1", "K1", "T0", "H3", "L2", "J3", "L1", "N1", "C0", "R1", "Q2", "Q1", "N0", "H2", "D0",
+        "K0", "L0", "J2", "J1", "M1", "Q0", "H1", "M0", "R0", "H0", "J0",
     ),
 )
+MERGE = ((1, 1), (0, 0))
 
 
 def kernel(cap, *refs):
@@ -74,18 +77,18 @@
 
 
 def body(cap, tok_hbm, gw_hbm, ids_hbm, wg_ref, wu_ref, wd_ref, out_ref,
-         tok_ref, gw_ref, ids_ref, xo, xa, yb, rows_in, cx, cy, rx, ry, tab, wgu, wdn, po, pin, mine, res,
-         rda, rdb, rcx, rcy, fx, fy, rfx, rfy, zs, zin, own, load_sem, ssem, rsem):
+         tok_ref, gw_ref, ids_ref, xo, xa, yb, rows_in, cx, cy, rx, ry, tab, near, seen, wgu, wdn, hid, po, pin, mine, res,
+         rda, rdb, rcx, rcy, fx, fy, rfx, rfy, zs, zin, zm, own, load_sem, ssem, rsem):
     ep = lax.axis_index("ep")
     core = lax.axis_index("half")
     x, y, z = ep % 2, (ep // 2) % 2, ep // 4
     tok, half = out_ref.shape
     part, rows, ff = half // 2, tok // 2, wg_ref.shape[2]
-    experts = tab.shape[2] // 2
+    experts = tab.shape[1] // 2
     nz = tab.shape[0]
     f32, bf = jnp.float32, jnp.bfloat16
     inner = ((z + 1) // 2) % 2
-    ex, ey = z * 4 + y * 2 + (1 - x), z * 4 + (1 - y) * 2 + x
+    ex, ey, ed = z * 4 + y * 2 + (1 - x), z * 4 + (1 - y) * 2 + x, z * 4 + (1 - y) * 2 + (1 - x)
     other, xn, yn = {"half": 1 - core}, {"ep": ex}, {"ep": ey}
     z1 = {"ep": (z + 1 - 2 * (z % 2)) * 4 + y * 2 + x}
     z3 = {"ep": (nz - 1 - z) * 4 + y * 2 + x}
@@ -146,25 +149,51 @@
         weight += jnp.where(hit, gw_ref[k : k + 1, :], 0.0)
     before = lax.broadcasted_iota(jnp.int32, (tok, tok), 0) < lax.broadcasted_iota(jnp.int32, (tok, tok), 1)
     rank = jnp.dot(chosen.astype(bf), jnp.where(before, 1.0, 0.0).astype(bf), preferred_element_type=f32)
-    tab[0, 0, 0:experts] = jnp.where(chosen > 0.0, rank, -1.0).astype(bf)
-    tab[0, 0, experts : 2 * experts] = weight.astype(bf)
+    tab[0, 0:experts] = jnp.where(chosen > 0.0, rank, -1.0).astype(bf)
+    tab[0, experts : 2 * experts] = weight.astype(bf)
 
     inputs[2].wait()
     pl.semaphore_wait(barrier, 4 + inner)
 
+    slot_at = lax.broadcasted_iota(jnp.int32, (cap, tok), 0).astype(f32)
+    tile_at = lax.broadcasted_iota(jnp.int32, (16, tok), 0)
+
+    def lookup(table, e, base):
+        half_of = table[base * experts : (base + 1) * experts].astype(f32)
+        return jnp.sum(jnp.where(expert_at == e, half_of, 0.0), axis=0, keepdims=True)
+
+    def row(d, line, who, base):
+        if line == 0:
+            return lookup(tab[d], {"me": ep, "x": ex, "y": ey}[who], base)
+        at = 2 * base + (who != "me")
+        return seen[d, line - 1].astype(f32)[at : at + 1]
+
+    def pick(d, line, es):
+        parts = [jnp.where(slot_at == row(d, line, e, 0), 1.0, 0.0).astype(bf) for e in es]
+        return jnp.concatenate(parts, axis=0)
+
+    def spread(d, line, e, values):
+        w = jnp.where(slot_at == row(d, line, e, 0), row(d, line, e, 1), 0.0)
+        return lax.dot_general(w.astype(bf), values, (((0,), (0,)), ((), ())), preferred_element_type=f32)
+
     def block(d):
         return tok_ref if d == 0 else xo.at[d - 1]
 
     def piece(d, p):
-        return tab.at[d, 0] if p == 2 else block(d).at[pl.ds(p * rows, rows)]
+        return tab.at[d] if p == 2 else block(d).at[pl.ds(p * rows, rows)]
 
     def hop(name, lands, p, came, to):
         return send((name, p), piece(came, p), piece(lands, p), to, ("z", lands, p))
 
     def plane(d, p):
         if p == 2:
-            go(("xt", d), tab.at[d, 0], tab.at[d, 1], xn)
-            go(("yt", d), tab.at[d, 0], tab.at[d, 2], yn)
+            for line, to, mark in ((1, xn, "xt"), (2, yn, "yt")):
+                tile = jnp.zeros((16, tok), f32)
+                for at, e in enumerate((ex if line == 1 else ey, ed)):
+                    for base in range(2):
+                        tile = jnp.where(tile_at == at + 2 * base, lookup(tab[d], e, base), tile)
+                near[d, line - 1] = tile.astype(bf)
+                go((mark, d), near.at[d, line - 1], seen.at[d, line - 1], to)
         else:
             here = pl.ds(p * rows, rows)
             go(("xf", d, p), block(d).at[here, left], xa.at[d, here], xn)
@@ -179,20 +208,6 @@
                 move(hop("z far", 1, p, 0, z3))
             plane(0, p)
 
-    slot_at = lax.broadcasted_iota(jnp.int32, (cap, tok), 0).astype(f32)
-
-    def row(d, line, e, base):
-        table = tab[d, line, base : base + experts].astype(f32)
-        return jnp.sum(jnp.where(expert_at == e, table, 0.0), axis=0, keepdims=True)
-
-    def pick(d, line, es):
-        parts = [jnp.where(slot_at == row(d, line, e, 0), 1.0, 0.0).astype(bf) for e in es]
-        return jnp.concatenate(parts, axis=0)
-
-    def spread(d, line, e, values):
-        w = jnp.where(slot_at == row(d, line, e, 0), row(d, line, e, experts), 0.0)
-        return lax.dot_general(w.astype(bf), values, (((0,), (0,)), ((), ())), preferred_element_type=f32)
-
     def expect(name, ref):
         send(name, ref, ref, other).wait_recv()
 
@@ -206,31 +221,33 @@
     c1, c2, c3, c4 = (pl.ds(i * cap, cap) for i in range(4))
     lo, hi = pl.ds(0, half), pl.ds(half, half)
 
-    def first(d):
-        got = jnp.dot(pick(d, 0, (ep, ey)), block(d)[:, left], preferred_element_type=f32).astype(bf)
+    def first_y(d):
+        got = jnp.dot(pick(d, 0, ("me", "y")), block(d)[:, left], preferred_element_type=f32).astype(bf)
         rows_in[d, c1, left] = got[:cap]
         cy[d] = got[cap:]
         go(("yc", d), cy.at[d], rows_in.at[d, c3, left], yn)
-        got = jnp.dot(pick(d, 0, (ep, ex)), block(d)[:, right], preferred_element_type=f32).astype(bf)
+
+    def first_x(d):
+        got = jnp.dot(pick(d, 0, ("me", "x")), block(d)[:, right], preferred_element_type=f32).astype(bf)
         rows_in[d, c1, right] = got[:cap]
         cx[d] = got[cap:]
         go(("xc", d), cx.at[d], rows_in.at[d, c2, right], xn)
         go(("g1", d), rows_in.at[d, c1, lo], rows_in.at[d, c1, hi], other)
 
     def cross_x(d):
-        expect(("xt", d), tab.at[d, 1])
+        expect(("xt", d), seen.at[d, 0])
         for p in range(2):
             expect(("xf", d, p), xa.at[d, pl.ds(p * rows, rows)])
-        got = jnp.dot(pick(d, 1, (ep, ey)), xa[d], preferred_element_type=f32).astype(bf)
+        got = jnp.dot(pick(d, 1, ("me", "y")), xa[d], preferred_element_type=f32).astype(bf)
         rows_in[d, c2, left] = got[:cap]
         ry[d] = got[cap:]
         go(("yr", d), ry.at[d], rows_in.at[d, c4, left], yn)
 
     def cross_y(d):
-        expect(("yt", d), tab.at[d, 2])
+        expect(("yt", d), seen.at[d, 1])
         for p in range(2):
             expect(("yf", d, p), yb.at[d, pl.ds(p * rows, rows)])
-        got = jnp.dot(pick(d, 2, (ep, ex)), yb[d], preferred_element_type=f32).astype(bf)
+        got = jnp.dot(pick(d, 2, ("me", "x")), yb[d], preferred_element_type=f32).astype(bf)
         rows_in[d, c3, right] = got[:cap]
         rx[d] = got[cap:]
         go(("xr", d), rx.at[d], rows_in.at[d, c4, right], xn)
@@ -253,10 +270,12 @@
         expect(("g3", d), rows_in.at[d, c4, hi])
         gu = jnp.dot(rows_in[d], wgu[...], preferred_element_type=f32)
         gate, up = gu[:, :ff], gu[:, ff:]
-        hidden = (gate / (1.0 + jnp.exp(-gate)) * up).astype(bf)
-        po[d] = jnp.dot(hidden, wdn[:, half:], preferred_element_type=f32).astype(bf)
+        hid[d] = (gate / (1.0 + jnp.exp(-gate)) * up).astype(bf)
+
+    def project(d):
+        po[d] = jnp.dot(hid[d], wdn[:, half:], preferred_element_type=f32).astype(bf)
         go(("p", d), po.at[d], pin.at[d], other)
-        mine[d] = jnp.dot(hidden, wdn[:, :half], preferred_element_type=f32).astype(bf)
+        mine[d] = jnp.dot(hid[d], wdn[:, :half], preferred_element_type=f32).astype(bf)
 
     def close(d):
         expect(("p", d), pin.at[d])
@@ -270,48 +289,66 @@
 
     def relay_x(d):
         expect(("da", d), rda.at[d])
-        fx[d] = (spread(d, 1, ep, res[d, c2, left]) + spread(d, 1, ey, rda[d])).astype(bf)
+        fx[d] = (spread(d, 1, "me", res[d, c2, left]) + spread(d, 1, "y", rda[d])).astype(bf)
         go(("fx", d), fx.at[d], rfx.at[d], xn)
 
     def relay_y(d):
         expect(("db", d), rdb.at[d])
-        fy[d] = (spread(d, 2, ep, res[d, c3, right]) + spread(d, 2, ex, rdb[d])).astype(bf)
+        fy[d] = (spread(d, 2, "me", res[d, c3, right]) + spread(d, 2, "x", rdb[d])).astype(bf)
         go(("fy", d), fy.at[d], rfy.at[d], yn)
 
     apart = (z + 1 - 2 * (z % 2), (z + 2) % nz, nz - 1 - z)
     def home(role, p, d):
         cols = right if p else left
-        e, part_in, full = (ex, rcx, rfy) if p else (ey, rcy, rfx)
+        e, part_in, full = ("x", rcx, rfy) if p else ("y", rcy, rfx)
         expect(("cx" if p else "cy", d), part_in.at[d])
         expect(("fy" if p else "fx", d), full.at[d])
-        total = spread(d, 0, ep, res[d, c1, cols]) + spread(d, 0, e, part_in[d]) + full[d].astype(f32)
+        total = spread(d, 0, "me", res[d, c1, cols]) + spread(d, 0, e, part_in[d]) + full[d].astype(f32)
         if d == 0:
             own[:, cols] = total
             return
         zs[d - 1, :, cols] = total.astype(bf)
+        if role == 0 and d > 1 and MERGE[d - 2][p]:
+            go(("o", d, p), zs.at[d - 1, :, cols], zm.at[d - 2, :, cols], z1, ("m", d, p))
+        elif role == 0 or not ((d == 1 and MERGE[0][p]) or (d == 3 and MERGE[1][p])):
+            forward(role, p, d)
+
+    def forward(role, p, d):
+        cols = right if p else left
         step = (d + 1) % 3 if role else d - 1
         go(("o", d, p), zs.at[d - 1, :, cols], zin.at[step, :, cols],
            {"ep": apart[step] * 4 + y * 2 + x}, ("s", step, p))
 
+    def merge(d, p):
+        at, cols = (0 if d == 1 else 1), right if p else left
+        if MERGE[at][p]:
+            expect(("m", at + 2, p), zm.at[at, :, cols])
+            zs[d - 1, :, cols] = (zs[d - 1, :, cols].astype(f32) + zm[at, :, cols].astype(f32)).astype(bf)
+            forward(1, p, d)
+
     def ready():
         for load in loads:
             load.wait()
 
-    def finish():
+    def finish(role):
         for p, cols in enumerate((left, right)):
             total = own[:, cols]
-            for d in range(nz - 1):
-                expect(("s", d, p), zin.at[d, :, cols])
-                total += zin[d, :, cols].astype(f32)
+            for step in range(nz - 1):
+                if (role == 0 and step == 2 and MERGE[1][p]) or (role == 1 and step == 1 and MERGE[0][p]):
+                    continue
+                expect(("s", step, p), zin.at[step, :, cols])
+                total += zin[step, :, cols].astype(f32)
             out_ref[:, cols] = total.astype(bf)
         for copy in sent:
             copy.wait_send()
         sent.clear()
 
     steps = {
-        "F": first, "X": cross_x, "Y": cross_y, "T": share_mid, "U": share_far, "C": compute, "W": ready,
-        "K": close, "L": direct, "R": relay_x, "Q": relay_y,
+        "F": first_y, "G": first_x, "X": cross_x, "Y": cross_y, "T": share_mid, "U": share_far, "W": ready,
+        "C": compute, "D": project, "K": close, "L": direct, "R": relay_x, "Q": relay_y,
+        "M": functools.partial(merge, 1), "N": functools.partial(merge, 3),
     }
+
     def step(role, word):
         at = [int(v) for v in word[1:]]
         if word[0] == "A":
@@ -327,7 +364,7 @@
             begin(role)
             for word in plan:
                 step(role, word)
-            finish()
+            finish(role)
 
 
 def multicast(tokens, gate_weights, expert_ids, w_gate, w_up, w_down):
@@ -342,7 +379,7 @@
     wide = pltpu.VMEM((nz, 4 * cap, half), bf)
     return pl.pallas_call(
         functools.partial(kernel, cap),
-        out_shape=jax.ShapeDtypeStruct((tok, half), bf),
+        out_shape=pltpu.VMEM((tok, half), bf),
         in_specs=[hbm] * 6,
         out_specs=vmem,
         scratch_shapes=[
@@ -352,14 +389,18 @@
             pltpu.VMEM((nz - 1, tok, half), bf), full, full,
             pltpu.VMEM((nz, 4 * cap, width), bf),
             compact, compact, compact, compact,
-            pltpu.VMEM((nz, 3, 2 * experts, tok), bf),
+            pltpu.VMEM((nz, 2 * experts, tok), bf),
+            pltpu.VMEM((nz, 2, 16, tok), bf),
+            pltpu.VMEM((nz, 2, 16, tok), bf),
             pltpu.VMEM((width, 2 * ff), bf),
             pltpu.VMEM((ff, width), bf),
+            pltpu.VMEM((nz, 4 * cap, ff), bf),
             wide, wide, wide, wide,
             compact, compact, compact, compact,
             full, full, full, full,
             pltpu.VMEM((nz - 1, tok, half), bf),
             pltpu.VMEM((nz - 1, tok, half), bf),
+            pltpu.VMEM((2, tok, half), bf),
             pltpu.VMEM((tok, half), jnp.float32),
         ],
         compiler_params=pltpu.CompilerParams(

time: 67.4 us -> 63.8 us (0.947)
  Pallas kernels: 65.5 us -> 62.9 us
  local copies, waits for them, and re-layouts: 1.67 us -> 0.71 us
    pallas_call x1, Pallas kernels: 65.5 us -> 62.9 us  [multicast(): pl.pallas_call(functools.partial(kernel, cap), out_shape=pltpu.VMEM((tok,...]
    unnamed x1, local copies, waits for them, and re-layouts: 1.67 us -> 0.71 us
where the time goes in v4:
time: 63.8 us; the launch traced here: 63.6 us
  Pallas kernels  62.9 us (99%)
  local copies, waits for them, and re-layouts  0.71 us (1%)
    pallas_call x1, Pallas kernels, multicast(): pl.pallas_call(functools.partial(kernel, cap), out_shape=pltpu.VMEM((tok,...  62.9 us

profile of v4, /device:TPU:0, one launch (start us, length us, event | category | flops | bytes accessed | tf_op | source)
XLA Modules:
  0.0 63.6 jit_solution(13326096143176997911)
XLA Ops:
  0.0 62.9 %shard_map.64 = bf16[128,1024]{1,0:T(8,128)(2,1)S(1)} custom-call(bf16[128,1024]{1,0:T(8,128)(2,1)} %refs_0_.1, f32[8,128]{1,0:T(8,128)} %bitcast.2, s32[8,128]{1,0:T(8,128)} %bitcast.3, bf16[1,2048,384]{2,1,0:T(8,128)(2,1)} %refs_3_.1, bf16[1,2048,384]{2,1,0:T(8,128)(2,1)} %refs_4_.1, bf16[1,384,2048]{2,1,0:T(8,128)(2,1)} %refs_5_.1), custom_call_target="tpu_custom_call" | custom-call | tf_op jit(solution)/shard_map/pallas_call | solution.py:380
  62.9 0.7 %copy.8 = bf16[128,1024]{1,0:T(8,128)(2,1)} copy(bf16[128,1024]{1,0:T(8,128)(2,1)S(1)} %shard_map.64) | data formatting | bytes 524288

commit v5 on v4

--- a/solution.py
+++ b/solution.py
@@ -54,31 +54,33 @@
 
 PLANS = (
     (
-        "A12", "F0", "G0", "Y0", "X0", "A10", "A11", "U0", "F1", "G1", "A22", "A20", "T0", "A21",
-        "F2", "G2", "A32", "A30", "X2", "Y2", "W", "C0", "A31", "F3", "G3", "U2", "T2", "Y3", "X3",
-        "X1", "C2", "T3", "D2", "Y1", "U3", "K2", "L2", "T1", "C3", "D3", "Q2", "K3", "R2", "U1",
-        "C1", "D1", "Q3", "L3", "J2", "K1", "R3", "H2", "D0", "J3", "Q1", "K0", "L1", "H3", "R1",
-        "J1", "Q0", "L0", "R0", "H1", "J0", "H0",
+        "A12", "F0", "G0", "A10", "Y0", "A22", "A11", "F1", "G1", "A20", "Y1", "X1", "A21", "F2",
+        "A32", "G2", "A30", "T1", "Y2", "U1", "X2", "A31", "W", "C1", "F3", "G3", "D1", "T2", "U2",
+        "Y3", "X3", "K1", "C2", "D2", "K2", "T3", "X0", "U3", "L2", "C3", "D3", "R2", "K3", "U0",
+        "Q2", "T0", "H20", "L3", "C0", "R3", "H21", "L1", "J20", "R1", "Q3", "D0", "J21", "K0",
+        "H30", "H31", "J30", "Q1", "J31", "L0", "H10", "J10", "R0", "Q0", "H11", "J11", "H00",
+        "J00", "H01", "J01",
     ),
     (
-        "A22", "F0", "A12", "A10", "A20", "A21", "A11", "A32", "A30", "F2", "G2", "A31", "X2", "Y2",
-        "F3", "G3", "T2", "X3", "X1", "X0", "Y3", "U2", "F1", "Y1", "G1", "G0", "T3", "W", "C2",
-        "U3", "Y0", "D2", "C3", "D3", "K2", "U1", "K3", "L3", "T1", "C1", "R3", "Q3", "U0", "R2",
-        "D1", "K1", "T0", "H3", "L2", "J3", "L1", "N1", "C0", "R1", "Q2", "Q1", "N0", "H2", "D0",
-        "K0", "L0", "J2", "J1", "M1", "Q0", "H1", "M0", "R0", "H0", "J0",
+        "A22", "F0", "G0", "A12", "A20", "A10", "A32", "A11", "A21", "F2", "A30", "G2", "Y2", "A31",
+        "X2", "Y1", "F1", "T2", "X1", "G1", "X0", "F3", "Y0", "Y3", "G3", "U2", "W", "C2", "X3",
+        "U1", "T1", "D2", "K2", "C1", "L2", "D1", "T0", "K1", "Q2", "R2", "U3", "L1", "T3", "U0",
+        "C3", "R1", "D3", "H20", "K3", "H21", "Q1", "L3", "J20", "C0", "H10", "R3", "M00", "D0",
+        "J21", "J10", "Q3", "K0", "H11", "M01", "M10", "H30", "N00", "L0", "H31", "N01", "J30",
+        "N10", "J31", "J11", "Q0", "N11", "R0", "M11", "J00", "H00", "J01", "H01",
     ),
 )
-MERGE = ((1, 1), (0, 0))
+MERGE = ((1, 1), (1, 1))
 
 
 def kernel(cap, *refs):
     dma = pltpu.SemaphoreType.DMA
-    pl.run_scoped(functools.partial(body, cap, *refs), dma((12,)), dma((136,)), dma((136,)))
+    pl.run_scoped(functools.partial(body, cap, *refs), dma((12,)), dma((180,)), dma((180,)))
 
 
 def body(cap, tok_hbm, gw_hbm, ids_hbm, wg_ref, wu_ref, wd_ref, out_ref,
          tok_ref, gw_ref, ids_ref, xo, xa, yb, rows_in, cx, cy, rx, ry, tab, near, seen, wgu, wdn, hid, po, pin, mine, res,
-         rda, rdb, rcx, rcy, fx, fy, rfx, rfy, zs, zin, zm, own, load_sem, ssem, rsem):
+         rda, rdb, rcx, rcy, fx, fy, rfx, rfy, zs, zin, zm, acc, own, load_sem, ssem, rsem):
     ep = lax.axis_index("ep")
     core = lax.axis_index("half")
     x, y, z = ep % 2, (ep // 2) % 2, ep // 4
@@ -272,59 +274,70 @@
         gate, up = gu[:, :ff], gu[:, ff:]
         hid[d] = (gate / (1.0 + jnp.exp(-gate)) * up).astype(bf)
 
+    rest = pl.ds(0, 3 * cap)
+
     def project(d):
         po[d] = jnp.dot(hid[d], wdn[:, half:], preferred_element_type=f32).astype(bf)
-        go(("p", d), po.at[d], pin.at[d], other)
+        go(("pf", d), po.at[d, c4], pin.at[d, c4], other)
+        go(("p", d), po.at[d, rest], pin.at[d, rest], other)
         mine[d] = jnp.dot(hid[d], wdn[:, :half], preferred_element_type=f32).astype(bf)
 
     def close(d):
-        expect(("p", d), pin.at[d])
-        res[d] = (mine[d].astype(f32) + pin[d].astype(f32)).astype(bf)
+        expect(("pf", d), pin.at[d, c4])
+        res[d, c4] = (mine[d, c4].astype(f32) + pin[d, c4].astype(f32)).astype(bf)
         go(("da", d), res.at[d, c4, left], rda.at[d], yn)
         go(("db", d), res.at[d, c4, right], rdb.at[d], xn)
 
     def direct(d):
+        expect(("p", d), pin.at[d, rest])
+        res[d, rest] = (mine[d, rest].astype(f32) + pin[d, rest].astype(f32)).astype(bf)
         go(("cy", d), res.at[d, c3, left], rcy.at[d], yn)
         go(("cx", d), res.at[d, c2, right], rcx.at[d], xn)
+
+    bands = {q: pl.ds(q * rows, rows) for q in range(2)}
 
     def relay_x(d):
         expect(("da", d), rda.at[d])
         fx[d] = (spread(d, 1, "me", res[d, c2, left]) + spread(d, 1, "y", rda[d])).astype(bf)
-        go(("fx", d), fx.at[d], rfx.at[d], xn)
+        for q in bands:
+            go(("fx", d, q), fx.at[d, bands[q]], rfx.at[d, bands[q]], xn)
 
     def relay_y(d):
         expect(("db", d), rdb.at[d])
         fy[d] = (spread(d, 2, "me", res[d, c3, right]) + spread(d, 2, "x", rdb[d])).astype(bf)
-        go(("fy", d), fy.at[d], rfy.at[d], yn)
+        for q in bands:
+            go(("fy", d, q), fy.at[d, bands[q]], rfy.at[d, bands[q]], yn)
 
     apart = (z + 1 - 2 * (z % 2), (z + 2) % nz, nz - 1 - z)
-    def home(role, p, d):
-        cols = right if p else left
+    def home(role, p, d, q):
+        cols, band = right if p else left, bands[q]
         e, part_in, full = ("x", rcx, rfy) if p else ("y", rcy, rfx)
-        expect(("cx" if p else "cy", d), part_in.at[d])
-        expect(("fy" if p else "fx", d), full.at[d])
-        total = spread(d, 0, "me", res[d, c1, cols]) + spread(d, 0, e, part_in[d]) + full[d].astype(f32)
+        if q == 0:
+            expect(("cx" if p else "cy", d), part_in.at[d])
+            acc[d, p] = spread(d, 0, "me", res[d, c1, cols]) + spread(d, 0, e, part_in[d])
+        expect(("fy" if p else "fx", d, q), full.at[d, band])
+        total = acc[d, p, band] + full[d, band].astype(f32)
         if d == 0:
-            own[:, cols] = total
+            own[band, cols] = total
             return
-        zs[d - 1, :, cols] = total.astype(bf)
+        zs[d - 1, band, cols] = total.astype(bf)
         if role == 0 and d > 1 and MERGE[d - 2][p]:
-            go(("o", d, p), zs.at[d - 1, :, cols], zm.at[d - 2, :, cols], z1, ("m", d, p))
+            go(("o", d, p, q), zs.at[d - 1, band, cols], zm.at[d - 2, band, cols], z1, ("m", d, p, q))
         elif role == 0 or not ((d == 1 and MERGE[0][p]) or (d == 3 and MERGE[1][p])):
-            forward(role, p, d)
-
-    def forward(role, p, d):
-        cols = right if p else left
+            forward(role, p, d, q)
+
+    def forward(role, p, d, q):
+        cols, band = right if p else left, bands[q]
         step = (d + 1) % 3 if role else d - 1
-        go(("o", d, p), zs.at[d - 1, :, cols], zin.at[step, :, cols],
-           {"ep": apart[step] * 4 + y * 2 + x}, ("s", step, p))
-
-    def merge(d, p):
-        at, cols = (0 if d == 1 else 1), right if p else left
+        go(("o", d, p, q), zs.at[d - 1, band, cols], zin.at[step, band, cols],
+           {"ep": apart[step] * 4 + y * 2 + x}, ("s", step, p, q))
+
+    def merge(d, p, q):
+        at, cols, band = (0 if d == 1 else 1), right if p else left, bands[q]
         if MERGE[at][p]:
-            expect(("m", at + 2, p), zm.at[at, :, cols])
-            zs[d - 1, :, cols] = (zs[d - 1, :, cols].astype(f32) + zm[at, :, cols].astype(f32)).astype(bf)
-            forward(1, p, d)
+            expect(("m", at + 2, p, q), zm.at[at, band, cols])
+            zs[d - 1, band, cols] = (zs[d - 1, band, cols].astype(f32) + zm[at, band, cols].astype(f32)).astype(bf)
+            forward(1, p, d, q)
 
     def ready():
         for load in loads:
@@ -336,7 +349,8 @@
             for step in range(nz - 1):
                 if (role == 0 and step == 2 and MERGE[1][p]) or (role == 1 and step == 1 and MERGE[0][p]):
                     continue
-                expect(("s", step, p), zin.at[step, :, cols])
+                for q in bands:
+                    expect(("s", step, p, q), zin.at[step, bands[q], cols])
                 total += zin[step, :, cols].astype(f32)
             out_ref[:, cols] = total.astype(bf)
         for copy in sent:
@@ -401,6 +415,7 @@
             pltpu.VMEM((nz - 1, tok, half), bf),
             pltpu.VMEM((nz - 1, tok, half), bf),
             pltpu.VMEM((2, tok, half), bf),
+            pltpu.VMEM((nz, 2, tok, part), jnp.float32),
             pltpu.VMEM((tok, half), jnp.float32),
         ],
         compiler_params=pltpu.CompilerParams(

time: 63.8 us -> 61.8 us (0.969)
  Pallas kernels: 62.9 us -> 60.9 us
    pallas_call x1, Pallas kernels: 62.9 us -> 60.9 us  [multicast(): pl.pallas_call(functools.partial(kernel, cap), out_shape=pltpu.VMEM((tok,...]
where the time goes in v5:
time: 61.8 us; the launch traced here: 61.6 us
  Pallas kernels  60.9 us (99%)
  local copies, waits for them, and re-layouts  0.71 us (1%)
    pallas_call x1, Pallas kernels, multicast(): pl.pallas_call(functools.partial(kernel, cap), out_shape=pltpu.VMEM((tok,...  60.9 us

profile of v5, /device:TPU:0, one launch (start us, length us, event | category | flops | bytes accessed | tf_op | source)
XLA Modules:
  0.0 61.6 jit_solution(3440035313900807327)
XLA Ops:
  0.0 60.9 %shard_map.64 = bf16[128,1024]{1,0:T(8,128)(2,1)S(1)} custom-call(bf16[128,1024]{1,0:T(8,128)(2,1)} %refs_0_.1, f32[8,128]{1,0:T(8,128)} %bitcast.2, s32[8,128]{1,0:T(8,128)} %bitcast.3, bf16[1,2048,384]{2,1,0:T(8,128)(2,1)} %refs_3_.1, bf16[1,2048,384]{2,1,0:T(8,128)(2,1)} %refs_4_.1, bf16[1,384,2048]{2,1,0:T(8,128)(2,1)} %refs_5_.1), custom_call_target="tpu_custom_call" | custom-call | tf_op jit(solution)/shard_map/pallas_call | solution.py:394
  60.9 0.7 %copy.8 = bf16[128,1024]{1,0:T(8,128)(2,1)} copy(bf16[128,1024]{1,0:T(8,128)(2,1)S(1)} %shard_map.64) | data formatting | bytes 524288

commit v6 on v5

--- a/solution.py
+++ b/solution.py
@@ -54,20 +54,22 @@
 
 PLANS = (
     (
-        "A12", "F0", "G0", "A10", "Y0", "A22", "A11", "F1", "G1", "A20", "Y1", "X1", "A21", "F2",
-        "A32", "G2", "A30", "T1", "Y2", "U1", "X2", "A31", "W", "C1", "F3", "G3", "D1", "T2", "U2",
-        "Y3", "X3", "K1", "C2", "D2", "K2", "T3", "X0", "U3", "L2", "C3", "D3", "R2", "K3", "U0",
-        "Q2", "T0", "H20", "L3", "C0", "R3", "H21", "L1", "J20", "R1", "Q3", "D0", "J21", "K0",
-        "H30", "H31", "J30", "Q1", "J31", "L0", "H10", "J10", "R0", "Q0", "H11", "J11", "H00",
-        "J00", "H01", "J01",
+        "A14", "F0", "G0", "A10", "X0", "Y0", "A11", "A24", "A12", "A13", "T0", "A20", "F1", "U0",
+        "G1", "A21", "W", "C0", "A22", "A23", "F2", "G2", "A34", "A30", "D0", "A31", "Y2", "X2",
+        "T2", "A32", "A33", "X1", "Y1", "U2", "F3", "G3", "Y3", "X3", "K0", "C2", "D2", "T1", "U1",
+        "K2", "T3", "L2", "U3", "C3", "R20", "Q20", "R21", "D3", "K3", "C1", "Q21", "L3", "J20",
+        "H20", "D1", "R30", "H21", "R31", "Q30", "J21", "K1", "H30", "Q31", "L1", "J30", "R10",
+        "Q10", "H31", "R11", "Q11", "L0", "J31", "H10", "J10", "Q00", "R00", "J11", "R01", "Q01",
+        "H11", "J00", "H00", "H01", "J01",
     ),
     (
-        "A22", "F0", "G0", "A12", "A20", "A10", "A32", "A11", "A21", "F2", "A30", "G2", "Y2", "A31",
-        "X2", "Y1", "F1", "T2", "X1", "G1", "X0", "F3", "Y0", "Y3", "G3", "U2", "W", "C2", "X3",
-        "U1", "T1", "D2", "K2", "C1", "L2", "D1", "T0", "K1", "Q2", "R2", "U3", "L1", "T3", "U0",
-        "C3", "R1", "D3", "H20", "K3", "H21", "Q1", "L3", "J20", "C0", "H10", "R3", "M00", "D0",
-        "J21", "J10", "Q3", "K0", "H11", "M01", "M10", "H30", "N00", "L0", "H31", "N01", "J30",
-        "N10", "J31", "J11", "Q0", "N11", "R0", "M11", "J00", "H00", "J01", "H01",
+        "A14", "A24", "A20", "A10", "A21", "A11", "A22", "A12", "A13", "F1", "G1", "A34", "A23",
+        "X1", "X0", "A30", "Y1", "A31", "X2", "F2", "A32", "T1", "Y2", "G2", "Y0", "U1", "A33", "W",
+        "C1", "F0", "F3", "D1", "U2", "G3", "G0", "T2", "X3", "U0", "Y3", "K1", "C2", "D2", "K2",
+        "U3", "T3", "L2", "L1", "Q10", "R20", "Q20", "R21", "Q21", "R10", "C3", "T0", "D3", "K3",
+        "C0", "H20", "Q11", "L3", "J20", "H10", "H21", "J10", "M10", "R30", "Q30", "M00", "R11",
+        "D0", "J11", "Q31", "J21", "M11", "R31", "H30", "N00", "K0", "L0", "J30", "N10", "H31",
+        "J31", "N01", "Q00", "N11", "Q01", "R00", "H11", "R01", "M01", "J00", "H00", "J01", "H01",
     ),
 )
 MERGE = ((1, 1), (1, 1))
@@ -75,7 +77,7 @@
 
 def kernel(cap, *refs):
     dma = pltpu.SemaphoreType.DMA
-    pl.run_scoped(functools.partial(body, cap, *refs), dma((12,)), dma((180,)), dma((180,)))
+    pl.run_scoped(functools.partial(body, cap, *refs), dma((12,)), dma((230,)), dma((230,)))
 
 
 def body(cap, tok_hbm, gw_hbm, ids_hbm, wg_ref, wu_ref, wd_ref, out_ref,
@@ -85,7 +87,7 @@
     core = lax.axis_index("half")
     x, y, z = ep % 2, (ep // 2) % 2, ep // 4
     tok, half = out_ref.shape
-    part, rows, ff = half // 2, tok // 2, wg_ref.shape[2]
+    part, rows, ff = half // 2, tok // 4, wg_ref.shape[2]
     experts = tab.shape[1] // 2
     nz = tab.shape[0]
     f32, bf = jnp.float32, jnp.bfloat16
@@ -182,13 +184,13 @@
         return tok_ref if d == 0 else xo.at[d - 1]
 
     def piece(d, p):
-        return tab.at[d] if p == 2 else block(d).at[pl.ds(p * rows, rows)]
+        return tab.at[d] if p == 4 else block(d).at[pl.ds(p * rows, rows)]
 
     def hop(name, lands, p, came, to):
         return send((name, p), piece(came, p), piece(lands, p), to, ("z", lands, p))
 
     def plane(d, p):
-        if p == 2:
+        if p == 4:
             for line, to, mark in ((1, xn, "xt"), (2, yn, "yt")):
                 tile = jnp.zeros((16, tok), f32)
                 for at, e in enumerate((ex if line == 1 else ey, ed)):
@@ -201,7 +203,7 @@
             go(("xf", d, p), block(d).at[here, left], xa.at[d, here], xn)
             go(("yf", d, p), block(d).at[here, right], yb.at[d, here], yn)
 
-    order = (2, 0, 1)
+    order = (4, 0, 1, 2, 3)
 
     def begin(role):
         for p in order:
@@ -238,7 +240,7 @@
 
     def cross_x(d):
         expect(("xt", d), seen.at[d, 0])
-        for p in range(2):
+        for p in range(4):
             expect(("xf", d, p), xa.at[d, pl.ds(p * rows, rows)])
         got = jnp.dot(pick(d, 1, ("me", "y")), xa[d], preferred_element_type=f32).astype(bf)
         rows_in[d, c2, left] = got[:cap]
@@ -247,7 +249,7 @@
 
     def cross_y(d):
         expect(("yt", d), seen.at[d, 1])
-        for p in range(2):
+        for p in range(4):
             expect(("yf", d, p), yb.at[d, pl.ds(p * rows, rows)])
         got = jnp.dot(pick(d, 2, ("me", "x")), yb[d], preferred_element_type=f32).astype(bf)
         rows_in[d, c3, right] = got[:cap]
@@ -275,6 +277,8 @@
         hid[d] = (gate / (1.0 + jnp.exp(-gate)) * up).astype(bf)
 
     rest = pl.ds(0, 3 * cap)
+    quarter = part // 2
+    bands = {q: pl.ds(q * quarter, quarter) for q in range(2)}
 
     def project(d):
         po[d] = jnp.dot(hid[d], wdn[:, half:], preferred_element_type=f32).astype(bf)
@@ -285,8 +289,9 @@
     def close(d):
         expect(("pf", d), pin.at[d, c4])
         res[d, c4] = (mine[d, c4].astype(f32) + pin[d, c4].astype(f32)).astype(bf)
-        go(("da", d), res.at[d, c4, left], rda.at[d], yn)
-        go(("db", d), res.at[d, c4, right], rdb.at[d], xn)
+        for q in bands:
+            go(("da", d, q), res.at[d, c4, bands[q]], rda.at[d, :, bands[q]], yn)
+            go(("db", d, q), res.at[d, c4, pl.ds(part + q * quarter, quarter)], rdb.at[d, :, bands[q]], xn)
 
     def direct(d):
         expect(("p", d), pin.at[d, rest])
@@ -294,49 +299,50 @@
         go(("cy", d), res.at[d, c3, left], rcy.at[d], yn)
         go(("cx", d), res.at[d, c2, right], rcx.at[d], xn)
 
-    bands = {q: pl.ds(q * rows, rows) for q in range(2)}
-
-    def relay_x(d):
-        expect(("da", d), rda.at[d])
-        fx[d] = (spread(d, 1, "me", res[d, c2, left]) + spread(d, 1, "y", rda[d])).astype(bf)
-        for q in bands:
-            go(("fx", d, q), fx.at[d, bands[q]], rfx.at[d, bands[q]], xn)
-
-    def relay_y(d):
-        expect(("db", d), rdb.at[d])
-        fy[d] = (spread(d, 2, "me", res[d, c3, right]) + spread(d, 2, "x", rdb[d])).astype(bf)
-        for q in bands:
-            go(("fy", d, q), fy.at[d, bands[q]], rfy.at[d, bands[q]], yn)
+    def relay_x(d, q):
+        expect(("da", d, q), rda.at[d, :, bands[q]])
+        fx[d, :, bands[q]] = (
+            spread(d, 1, "me", res[d, c2, bands[q]]) + spread(d, 1, "y", rda[d, :, bands[q]])
+        ).astype(bf)
+        go(("fx", d, q), fx.at[d, :, bands[q]], rfx.at[d, :, bands[q]], xn)
+
+    def relay_y(d, q):
+        expect(("db", d, q), rdb.at[d, :, bands[q]])
+        here = pl.ds(part + q * quarter, quarter)
+        fy[d, :, bands[q]] = (
+            spread(d, 2, "me", res[d, c3, here]) + spread(d, 2, "x", rdb[d, :, bands[q]])
+        ).astype(bf)
+        go(("fy", d, q), fy.at[d, :, bands[q]], rfy.at[d, :, bands[q]], yn)
 
     apart = (z + 1 - 2 * (z % 2), (z + 2) % nz, nz - 1 - z)
     def home(role, p, d, q):
-        cols, band = right if p else left, bands[q]
+        band, here = bands[q], pl.ds(p * part + q * quarter, quarter)
         e, part_in, full = ("x", rcx, rfy) if p else ("y", rcy, rfx)
         if q == 0:
             expect(("cx" if p else "cy", d), part_in.at[d])
-            acc[d, p] = spread(d, 0, "me", res[d, c1, cols]) + spread(d, 0, e, part_in[d])
-        expect(("fy" if p else "fx", d, q), full.at[d, band])
-        total = acc[d, p, band] + full[d, band].astype(f32)
+            acc[d, p] = spread(d, 0, "me", res[d, c1, right if p else left]) + spread(d, 0, e, part_in[d])
+        expect(("fy" if p else "fx", d, q), full.at[d, :, band])
+        total = acc[d, p, :, band] + full[d, :, band].astype(f32)
         if d == 0:
-            own[band, cols] = total
+            own[:, here] = total
             return
-        zs[d - 1, band, cols] = total.astype(bf)
+        zs[d - 1, :, here] = total.astype(bf)
         if role == 0 and d > 1 and MERGE[d - 2][p]:
-            go(("o", d, p, q), zs.at[d - 1, band, cols], zm.at[d - 2, band, cols], z1, ("m", d, p, q))
+            go(("o", d, p, q), zs.at[d - 1, :, here], zm.at[d - 2, :, here], z1, ("m", d, p, q))
         elif role == 0 or not ((d == 1 and MERGE[0][p]) or (d == 3 and MERGE[1][p])):
             forward(role, p, d, q)
 
     def forward(role, p, d, q):
-        cols, band = right if p else left, bands[q]
+        here = pl.ds(p * part + q * quarter, quarter)
         step = (d + 1) % 3 if role else d - 1
-        go(("o", d, p, q), zs.at[d - 1, band, cols], zin.at[step, band, cols],
+        go(("o", d, p, q), zs.at[d - 1, :, here], zin.at[step, :, here],
            {"ep": apart[step] * 4 + y * 2 + x}, ("s", step, p, q))
 
     def merge(d, p, q):
-        at, cols, band = (0 if d == 1 else 1), right if p else left, bands[q]
+        at, here = (0 if d == 1 else 1), pl.ds(p * part + q * quarter, quarter)
         if MERGE[at][p]:
-            expect(("m", at + 2, p, q), zm.at[at, band, cols])
-            zs[d - 1, band, cols] = (zs[d - 1, band, cols].astype(f32) + zm[at, band, cols].astype(f32)).astype(bf)
+            expect(("m", at + 2, p, q), zm.at[at, :, here])
+            zs[d - 1, :, here] = (zs[d - 1, :, here].astype(f32) + zm[at, :, here].astype(f32)).astype(bf)
             forward(1, p, d, q)
 
     def ready():
@@ -350,7 +356,8 @@
                 if (role == 0 and step == 2 and MERGE[1][p]) or (role == 1 and step == 1 and MERGE[0][p]):
                     continue
                 for q in bands:
-                    expect(("s", step, p, q), zin.at[step, bands[q], cols])
+                    here = pl.ds(p * part + q * quarter, quarter)
+                    expect(("s", step, p, q), zin.at[step, :, here])
                 total += zin[step, :, cols].astype(f32)
             out_ref[:, cols] = total.astype(bf)
         for copy in sent:

time: 61.8 us -> 60.5 us (0.979)
  Pallas kernels: 60.9 us -> 59.6 us
    pallas_call x1, Pallas kernels: 60.9 us -> 59.6 us  [multicast(): pl.pallas_call(functools.partial(kernel, cap), out_shape=pltpu.VMEM((tok,...]
where the time goes in v6:
time: 60.5 us; the launch traced here: 60.3 us
  Pallas kernels  59.6 us (99%)
  local copies, waits for them, and re-layouts  0.71 us (1%)
    pallas_call x1, Pallas kernels, multicast(): pl.pallas_call(functools.partial(kernel, cap), out_shape=pltpu.VMEM((tok,...  59.6 us

profile of v6, /device:TPU:0, one launch (start us, length us, event | category | flops | bytes accessed | tf_op | source)
XLA Modules:
  0.0 60.3 jit_solution(15012573868872270443)
XLA Ops:
  0.0 59.6 %shard_map.64 = bf16[128,1024]{1,0:T(8,128)(2,1)S(1)} custom-call(bf16[128,1024]{1,0:T(8,128)(2,1)} %refs_0_.1, f32[8,128]{1,0:T(8,128)} %bitcast.2, s32[8,128]{1,0:T(8,128)} %bitcast.3, bf16[1,2048,384]{2,1,0:T(8,128)(2,1)} %refs_3_.1, bf16[1,2048,384]{2,1,0:T(8,128)(2,1)} %refs_4_.1, bf16[1,384,2048]{2,1,0:T(8,128)(2,1)} %refs_5_.1), custom_call_target="tpu_custom_call" | custom-call | tf_op jit(solution)/shard_map/pallas_call | solution.py:401
  59.6 0.7 %copy.8 = bf16[128,1024]{1,0:T(8,128)(2,1)} copy(bf16[128,1024]{1,0:T(8,128)(2,1)S(1)} %shard_map.64) | data formatting | bytes 524288

commit v7 on v6

--- a/solution.py
+++ b/solution.py
@@ -54,22 +54,23 @@
 
 PLANS = (
     (
-        "A14", "F0", "G0", "A10", "X0", "Y0", "A11", "A24", "A12", "A13", "T0", "A20", "F1", "U0",
-        "G1", "A21", "W", "C0", "A22", "A23", "F2", "G2", "A34", "A30", "D0", "A31", "Y2", "X2",
-        "T2", "A32", "A33", "X1", "Y1", "U2", "F3", "G3", "Y3", "X3", "K0", "C2", "D2", "T1", "U1",
-        "K2", "T3", "L2", "U3", "C3", "R20", "Q20", "R21", "D3", "K3", "C1", "Q21", "L3", "J20",
-        "H20", "D1", "R30", "H21", "R31", "Q30", "J21", "K1", "H30", "Q31", "L1", "J30", "R10",
-        "Q10", "H31", "R11", "Q11", "L0", "J31", "H10", "J10", "Q00", "R00", "J11", "R01", "Q01",
-        "H11", "J00", "H00", "H01", "J01",
+        "F0", "G0", "A14", "A10", "A11", "X0", "A12", "Y0", "A24", "A13", "F1", "T0", "A20", "G1",
+        "A21", "A22", "A23", "F2", "G2", "A34", "A30", "Y2", "A31", "X2", "U0", "T2", "A32", "A33",
+        "W", "C0", "F3", "G3", "U2", "X3", "Y3", "C2", "X1", "Y1", "D2", "T3", "K2", "U3", "L2",
+        "T1", "C3", "U1", "Q20", "R20", "D3", "R21", "Q21", "K3", "C1", "H20", "L3", "D1", "Q30",
+        "K1", "H21", "R30", "J20", "D0", "J21", "R31", "Q31", "L1", "J30", "H30", "R10", "R11",
+        "K0", "Q10", "Q11", "J31", "H31", "H10", "L0", "H11", "R00", "J10", "R01", "Q00", "J11",
+        "Q01", "H00", "J00", "H01", "J01",
     ),
     (
-        "A14", "A24", "A20", "A10", "A21", "A11", "A22", "A12", "A13", "F1", "G1", "A34", "A23",
-        "X1", "X0", "A30", "Y1", "A31", "X2", "F2", "A32", "T1", "Y2", "G2", "Y0", "U1", "A33", "W",
-        "C1", "F0", "F3", "D1", "U2", "G3", "G0", "T2", "X3", "U0", "Y3", "K1", "C2", "D2", "K2",
-        "U3", "T3", "L2", "L1", "Q10", "R20", "Q20", "R21", "Q21", "R10", "C3", "T0", "D3", "K3",
-        "C0", "H20", "Q11", "L3", "J20", "H10", "H21", "J10", "M10", "R30", "Q30", "M00", "R11",
-        "D0", "J11", "Q31", "J21", "M11", "R31", "H30", "N00", "K0", "L0", "J30", "N10", "H31",
-        "J31", "N01", "Q00", "N11", "Q01", "R00", "H11", "R01", "M01", "J00", "H00", "J01", "H01",
+        "F0", "A24", "A14", "G0", "A20", "A10", "A11", "A21", "A22", "A23", "A12", "F2", "A13",
+        "A34", "G2", "F1", "A30", "A31", "G1", "Y1", "X1", "A32", "A33", "Y2", "T1", "X2", "U1",
+        "F3", "G3", "Y3", "T2", "W", "C1", "Y0", "U2", "X0", "D1", "X3", "T0", "K1", "C2", "L1",
+        "D2", "K2", "T3", "Q10", "R10", "U3", "L2", "C3", "D3", "R11", "K3", "U0", "R20", "Q20",
+        "L3", "H10", "C0", "J10", "M00", "R21", "Q30", "Q21", "H11", "J20", "R30", "Q31", "M01",
+        "D0", "H20", "M10", "K0", "Q11", "H21", "R31", "J30", "N10", "H30", "N00", "L0", "R00",
+        "J31", "N11", "H31", "N01", "J21", "R01", "Q00", "J11", "Q01", "M11", "H00", "J00", "J01",
+        "H01",
     ),
 )
 MERGE = ((1, 1), (1, 1))
@@ -300,18 +301,15 @@
         go(("cx", d), res.at[d, c2, right], rcx.at[d], xn)
 
     def relay_x(d, q):
+        ours = spread(d, 1, "me", res[d, c2, bands[q]])
         expect(("da", d, q), rda.at[d, :, bands[q]])
-        fx[d, :, bands[q]] = (
-            spread(d, 1, "me", res[d, c2, bands[q]]) + spread(d, 1, "y", rda[d, :, bands[q]])
-        ).astype(bf)
+        fx[d, :, bands[q]] = (ours + spread(d, 1, "y", rda[d, :, bands[q]])).astype(bf)
         go(("fx", d, q), fx.at[d, :, bands[q]], rfx.at[d, :, bands[q]], xn)
 
     def relay_y(d, q):
+        ours = spread(d, 2, "me", res[d, c3, pl.ds(part + q * quarter, quarter)])
         expect(("db", d, q), rdb.at[d, :, bands[q]])
-        here = pl.ds(part + q * quarter, quarter)
-        fy[d, :, bands[q]] = (
-            spread(d, 2, "me", res[d, c3, here]) + spread(d, 2, "x", rdb[d, :, bands[q]])
-        ).astype(bf)
+        fy[d, :, bands[q]] = (ours + spread(d, 2, "x", rdb[d, :, bands[q]])).astype(bf)
         go(("fy", d, q), fy.at[d, :, bands[q]], rfy.at[d, :, bands[q]], yn)
 
     apart = (z + 1 - 2 * (z % 2), (z + 2) % nz, nz - 1 - z)
@@ -319,8 +317,9 @@
         band, here = bands[q], pl.ds(p * part + q * quarter, quarter)
         e, part_in, full = ("x", rcx, rfy) if p else ("y", rcy, rfx)
         if q == 0:
+            ours = spread(d, 0, "me", res[d, c1, right if p else left])
             expect(("cx" if p else "cy", d), part_in.at[d])
-            acc[d, p] = spread(d, 0, "me", res[d, c1, right if p else left]) + spread(d, 0, e, part_in[d])
+            acc[d, p] = ours + spread(d, 0, e, part_in[d])
         expect(("fy" if p else "fx", d, q), full.at[d, :, band])
         total = acc[d, p, :, band] + full[d, :, band].astype(f32)
         if d == 0:

time: 60.5 us -> 60.5 us (level)
  no operation moved by 1% of the time
where the time goes in v7:
time: 60.5 us; the launch traced here: 60.4 us
  Pallas kernels  59.6 us (99%)
  local copies, waits for them, and re-layouts  0.71 us (1%)
    pallas_call x1, Pallas kernels, multicast(): pl.pallas_call(functools.partial(kernel, cap), out_shape=pltpu.VMEM((tok,...  59.6 us

profile of v7, /device:TPU:0, one launch (start us, length us, event | category | flops | bytes accessed | tf_op | source)
XLA Modules:
  0.0 60.4 jit_solution(16410316160496978437)
XLA Ops:
  0.0 59.6 %shard_map.64 = bf16[128,1024]{1,0:T(8,128)(2,1)S(1)} custom-call(bf16[128,1024]{1,0:T(8,128)(2,1)} %refs_0_.1, f32[8,128]{1,0:T(8,128)} %bitcast.2, s32[8,128]{1,0:T(8,128)} %bitcast.3, bf16[1,2048,384]{2,1,0:T(8,128)(2,1)} %refs_3_.1, bf16[1,2048,384]{2,1,0:T(8,128)(2,1)} %refs_4_.1, bf16[1,384,2048]{2,1,0:T(8,128)(2,1)} %refs_5_.1), custom_call_target="tpu_custom_call" | custom-call | tf_op jit(solution)/shard_map/pallas_call | solution.py:400
  59.6 0.7 %copy.8 = bf16[128,1024]{1,0:T(8,128)(2,1)} copy(bf16[128,1024]{1,0:T(8,128)(2,1)S(1)} %shard_map.64) | data formatting | bytes 524288
